TPU v7x, 8 devices: a whole 2x2x1 slice. The times are simulated.
8 devices in a mesh: dp: 2 (over z, y), sp: 4 (over x, core).
Axes of the slice: x: 2, y: 2, z: 1, core: 2. Of those that a mesh axis runs over, the one named last changes fastest.
Arguments:
- latent: bfloat16 [32, 64, 64, 4], P('dp', 'sp'), parts along dimension 0
- time_emb: bfloat16 [32, 1280], P('dp'), parts along dimension 0
- w_in: bfloat16 [3, 3, 4, 320], replicated
- b_in: bfloat16 [320], replicated
- gn1_scale: bfloat16 [2, 320], replicated
- gn1_shift: bfloat16 [2, 320], replicated
- conv1_w: bfloat16 [2, 3, 3, 320, 320], replicated
- conv1_b: bfloat16 [2, 320], replicated
- temb_w: bfloat16 [2, 1280, 320], replicated
- temb_b: bfloat16 [2, 320], replicated
- gn2_scale: bfloat16 [2, 320], replicated
- gn2_shift: bfloat16 [2, 320], replicated
- conv2_w: bfloat16 [2, 3, 3, 320, 320], replicated
- conv2_b: bfloat16 [2, 320], replicated
- down_w: bfloat16 [3, 3, 320, 320], replicated
- down_b: bfloat16 [320], replicated
Outputs:
- output 1: bfloat16 [32, 64, 64, 320], P('dp', 'sp'), parts along dimension 0
- output 2: bfloat16 [32, 64, 64, 320], P('dp', 'sp'), parts along dimension 0
- output 3: bfloat16 [32, 64, 64, 320], P('dp', 'sp'), parts along dimension 0
- output 4: bfloat16 [32, 32, 32, 320], P('dp', 'sp'), parts along dimension 0
There are 2 independent parts. A program takes and returns all parts, laid end to end along the dimension named above; an argument that names none is the same for every part.
All inputs are finite; a program needn't handle non-finite values.
Results may differ from a plain program's by a relative error of at most 0.0134557.
Values are sent between devices in bfloat16 or wider.
A program may use at most 1 GiB of HBM per device.

v0:
```python
import jax
import jax.numpy as jnp
from jax import lax
from jax.sharding import PartitionSpec as P

GN_GROUPS = 32
GN_EPS = 1e-5
DIM_NUMS = ("NHWC", "HWIO", "NHWC")


def conv_valid_rows(inputs, kernel, bias_c, stride):
    out_f32 = lax.conv_general_dilated(inputs, kernel, (stride, stride), ((0, 0), (1, 1)), dimension_numbers=DIM_NUMS, preferred_element_type=jnp.float32)
    return (out_f32 + bias_c.astype(jnp.float32)).astype(jnp.bfloat16)


def group_sums(values):
    batch_n, rows_n, cols_n, chan_n = values.shape
    grouped = values.reshape(batch_n, rows_n * cols_n, GN_GROUPS, chan_n // GN_GROUPS)
    return jnp.stack([grouped.sum(axis=(1, 3)), jnp.square(grouped).sum(axis=(1, 3))], axis=-1)


def norm_silu(values, sums_all, elem_count, gain_c, shift_c):
    group_ch = values.shape[-1] // GN_GROUPS
    grp_mean = sums_all[..., 0] / elem_count
    grp_var = sums_all[..., 1] / elem_count - grp_mean * grp_mean
    inv_std = lax.rsqrt(grp_var + GN_EPS)
    scale_bc = jnp.repeat(inv_std, group_ch, axis=1) * gain_c.astype(jnp.float32)
    offset_bc = shift_c.astype(jnp.float32) - jnp.repeat(grp_mean, group_ch, axis=1) * scale_bc
    return jax.nn.silu(values * scale_bc[:, None, None, :] + offset_bc[:, None, None, :]).astype(jnp.bfloat16)


def solution(mesh):
    sp_size = mesh.shape["sp"]
    to_next = [(device, device + 1) for device in range(sp_size - 1)]
    to_prev = [(device + 1, device) for device in range(sp_size - 1)]

    def row_from_above(band_block):
        return lax.ppermute(band_block[:, -1:], "sp", to_next)

    def row_from_below(band_block):
        return lax.ppermute(band_block[:, :1], "sp", to_prev)

    def conv_band(band_block, kernel, bias_c):
        padded = jnp.concatenate([row_from_above(band_block), band_block, row_from_below(band_block)], axis=1)
        return conv_valid_rows(padded, kernel, bias_c, 1)

    def band_program(latent, time_emb, w_in, b_in, gn1_scale, gn1_shift, conv1_w, conv1_b, temb_w, temb_b, gn2_scale, gn2_shift, conv2_w, conv2_b, down_w, down_b):
        elem_count = latent.shape[1] * sp_size * latent.shape[2] * (w_in.shape[-1] // GN_GROUPS)
        emb_act = jax.nn.silu(time_emb.astype(jnp.float32)).astype(jnp.bfloat16)
        hidden = conv_band(latent, w_in, b_in)
        outputs = [hidden]
        for layer_idx in range(conv1_w.shape[0]):
            hidden_f32 = hidden.astype(jnp.float32)
            sums_all = lax.psum(group_sums(hidden_f32), "sp")
            normed = norm_silu(hidden_f32, sums_all, elem_count, gn1_scale[layer_idx], gn1_shift[layer_idx])
            branch = conv_band(normed, conv1_w[layer_idx], conv1_b[layer_idx])
            emb_proj = jnp.dot(emb_act, temb_w[layer_idx], preferred_element_type=jnp.float32) + temb_b[layer_idx].astype(jnp.float32)
            mixed_in = branch.astype(jnp.float32) + emb_proj[:, None, None, :]
            sums_all = lax.psum(group_sums(mixed_in), "sp")
            normed = norm_silu(mixed_in, sums_all, elem_count, gn2_scale[layer_idx], gn2_shift[layer_idx])
            branch = conv_band(normed, conv2_w[layer_idx], conv2_b[layer_idx])
            hidden = (hidden_f32 + branch.astype(jnp.float32)).astype(jnp.bfloat16)
            outputs.append(hidden)
        padded = jnp.concatenate([row_from_above(hidden), hidden], axis=1)
        outputs.append(conv_valid_rows(padded, down_w, down_b, 2))
        return tuple(outputs)

    band_spec = P("dp", "sp", None, None)
    return jax.shard_map(band_program, mesh=mesh, in_specs=(band_spec, P("dp", None)) + (P(),) * 14, out_specs=(band_spec,) * 4, check_vma=False)
```

profile of v0, /device:TPU:0, one launch (start us, length us, event | category | flops | bytes accessed | tf_op | source)
XLA Modules:
  0.0 468.7 jit_solution(9115757761824668150)
XLA Ops:
  0.6 2.0 copy.42
  2.7 2.8 collective-permute-start
  5.5 1.3 collective-permute-start.1
  6.8 1.4 convert_reduce_fusion.7
  8.2 0.7 convert_element_type.126
  8.9 1.9 collective-permute-done.1
  10.8 12.0 %convert_reduce_fusion.1 = (f32[16,320]{1,0:T(8,128)S(1)}, f32[16,320]{1,0:T(8,128)S(1)}, bf16[16,16,64,320]{3,0,2,1:T(8,128)(2,1)}) fusion(f32[320]{0:T(512)S(1)} %convert_element_type.126, bf16[3,3,4,320]{3,2,1,0:T(4,128)(2,1)} %param.18, bf16[16,1,64,4]{0,3,2,1:T(4,128)(2,1)S(1)} %collective-permute-done.1, bf16[16,16,64,4]{0,3,2,1:T(4,128)(2,1)S(1)} %copy.42, ...), kind=kOutput, calls=%fused_computation.7 | convolution fusion | flops 405444608 | bytes 10698496 | tf_op jit(solution)/shard_map/conv_general_dilated | solution.py:12
  22.7 0.3 reduce_sum.96
  23.0 0.3 reduce_sum.99
  23.6 12.9 %psum.28 = f32[16,32,2]{1,0,2:T(8,128)S(1)} all-reduce(f32[16,32,2]{1,0,2:T(8,128)S(1)} %pad_maximum_fusion), channel_id=1, replica_groups=mesh['dp'=2,'sp'=4] {'sp'}, use_global_device_ids=true, to_apply=%region_4.5 | all-reduce | flops 1024 | bytes 8192 | tf_op jit(solution)/shard_map/psum | solution.py:54
  36.6 0.2 reshape.300
  36.9 0.2 reshape.301
  37.2 10.0 %fusion.7 = bf16[16,16,64,320]{3,0,2,1:T(8,128)(2,1)S(1)} fusion(bf16[16,16,64,320]{3,0,2,1:T(8,128)(2,1)} %get-tuple-element.60, f32[16,320]{1,0:T(8,128)S(1)} %get-tuple-element.48, f32[16,320]{1,0:T(8,128)S(1)} %get-tuple-element.49), kind=kLoop, calls=%fused_computation.15 | loop fusion | flops 41943040 | bytes 21012480 | tf_op jit(solution)/shard_map/convert_element_type | solution.py:29
  47.4 1.4 collective-permute-start.2
  48.8 1.3 collective-permute-start.3
  50.1 0.6 convert_reduce_fusion.6
  50.7 0.6 convert_reduce_fusion.5
  51.3 0.6 convert_reduce_fusion.3
  51.9 0.3 convolution_add_fusion.1
  52.3 2.5 collective-permute-done.3
  54.7 58.6 %fusion.19 = (f32[16,320]{1,0:T(8,128)S(1)}, f32[16,320]{1,0:T(8,128)S(1)}, bf16[16,16,64,320]{3,0,2,1:T(8,128)(2,1)}) fusion(f32[16,320]{1,0:T(8,128)S(1)} %convolution_add_fusion.1, f32[320]{0:T(512)S(1)} %get-tuple-element.39, bf16[2,3,3,320,320]{4,3,2,1,0:T(8,128)(2,1)} %param.22, bf16[16,1,64,320]{3,0,2,1:T(8,128)(2,1)S(1)} %collective-permute-done.3, ...), kind=kOutput, calls=%fused_computation.36 | convolution fusion | flops 29956497408 | bytes 24556800 | tf_op jit(solution)/shard_map/conv_general_dilated | solution.py:12
  113.3 0.3 reduce_sum.105
  113.7 0.3 reduce_sum.111
  114.2 19.6 %psum.29 = f32[16,32,2]{1,0,2:T(8,128)S(1)} all-reduce(f32[16,32,2]{1,0,2:T(8,128)S(1)} %pad_maximum_fusion.1), channel_id=1, replica_groups=mesh['dp'=2,'sp'=4] {'sp'}, use_global_device_ids=true, to_apply=%region_9.10 | all-reduce | flops 1024 | bytes 8192 | tf_op jit(solution)/shard_map/psum | solution.py:59
  133.9 0.2 reshape.302
  134.2 0.2 reshape.303
  134.4 10.4 %multiply_convert_fusion.1 = bf16[16,16,64,320]{3,0,2,1:T(8,128)(2,1)S(1)} fusion(bf16[16,16,64,320]{3,0,2,1:T(8,128)(2,1)} %get-tuple-element.61, f32[16,320]{1,0:T(8,128)S(1)} %get-tuple-element.46, f32[16,320]{1,0:T(8,128)S(1)} %get-tuple-element.47, f32[16,320]{1,0:T(8,128)S(1)} %convolution_add_fusion.1), kind=kLoop, calls=%fused_computation.33 | loop fusion | flops 47185920 | bytes 21032960 | tf_op jit(solution)/shard_map/convert_element_type | solution.py:29
  144.8 0.2 fusion.109
  145.0 1.4 collective-permute-start.4
  146.4 1.3 collective-permute-start.5
  147.7 0.6 convert_reduce_fusion.2
  148.3 4.0 collective-permute-done.5
  152.3 60.6 %convert_reduce_fusion = (f32[16,320]{1,0:T(8,128)S(1)}, f32[16,320]{1,0:T(8,128)S(1)}, bf16[16,16,64,320]{3,0,2,1:T(8,128)(2,1)}) fusion(f32[320]{0:T(512)S(1)} %get-tuple-element.41, bf16[2,3,3,320,320]{4,3,2,1,0:T(8,128)(2,1)} %param.28, bf16[16,1,64,320]{3,0,2,1:T(8,128)(2,1)S(1)} %collective-permute-done.5, ...), kind=kOutput, calls=%fused_computation.3 | convolution fusion | flops 29972226048 | bytes 37119232 | tf_op jit(solution)/shard_map/conv_general_dilated | solution.py:12
  212.9 0.3 reduce_sum.114
  213.3 0.3 reduce_sum.144
  213.7 19.6 %psum.30 = f32[16,32,2]{1,0,2:T(8,128)S(1)} all-reduce(f32[16,32,2]{1,0,2:T(8,128)S(1)} %pad_maximum_fusion.2), channel_id=1, replica_groups=mesh['dp'=2,'sp'=4] {'sp'}, use_global_device_ids=true, to_apply=%region_14.15 | all-reduce | flops 1024 | bytes 8192 | tf_op jit(solution)/shard_map/psum | solution.py:54
  233.5 0.2 reshape.304
  233.8 0.2 reshape.305
  234.1 10.1 %fusion.16 = bf16[16,16,64,320]{3,0,2,1:T(8,128)(2,1)S(1)} fusion(bf16[16,16,64,320]{3,0,2,1:T(8,128)(2,1)} %get-tuple-element.62, f32[16,320]{1,0:T(8,128)S(1)} %get-tuple-element.44, f32[16,320]{1,0:T(8,128)S(1)} %get-tuple-element.45), kind=kLoop, calls=%fused_computation.24 | loop fusion | flops 41943040 | bytes 21012480 | tf_op jit(solution)/shard_map/convert_element_type | solution.py:29
  244.3 1.4 collective-permute-start.6
  245.7 1.3 collective-permute-start.7
  247.1 0.3 convolution_add_fusion
  247.4 0.2 collective-permute-done.6
  247.6 4.1 collective-permute-done.7
  251.7 57.2 %fusion.18 = (f32[16,320]{1,0:T(8,128)S(1)}, f32[16,320]{1,0:T(8,128)S(1)}, bf16[16,16,64,320]{3,0,2,1:T(8,128)(2,1)}) fusion(f32[16,320]{1,0:T(8,128)S(1)} %convolution_add_fusion, f32[320]{0:T(512)S(1)} %copy-done.11, bf16[2,3,3,320,320]{4,3,2,1,0:T(8,128)(2,1)S(1)} %copy-done.15, bf16[16,1,64,320]{3,0,2,1:T(8,128)(2,1)S(1)} %collective-permute-done.7, ...), kind=kOutput, calls=%fused_computation.30 | convolution fusion | flops 29956497408 | bytes 26920960 | tf_op jit(solution)/shard_map/conv_general_dilated | solution.py:12
  308.9 0.3 reduce_sum.147
  309.3 0.3 reduce_sum.150
  309.8 19.6 %psum.31 = f32[16,32,2]{1,0,2:T(8,128)S(1)} all-reduce(f32[16,32,2]{1,0,2:T(8,128)S(1)} %pad_maximum_fusion.3), channel_id=1, replica_groups=mesh['dp'=2,'sp'=4] {'sp'}, use_global_device_ids=true, to_apply=%region_19.20 | all-reduce | flops 1024 | bytes 8192 | tf_op jit(solution)/shard_map/psum | solution.py:59
  329.5 0.2 reshape.306
  329.8 0.2 reshape.307
  330.1 11.1 %multiply_convert_fusion = bf16[16,16,64,320]{3,0,2,1:T(8,128)(2,1)S(1)} fusion(bf16[16,16,64,320]{3,0,2,1:T(8,128)(2,1)} %get-tuple-element.63, f32[16,320]{1,0:T(8,128)S(1)} %get-tuple-element.42, f32[16,320]{1,0:T(8,128)S(1)} %get-tuple-element.43, f32[16,320]{1,0:T(8,128)S(1)} %convolution_add_fusion), kind=kLoop, calls=%fused_computation.27 | loop fusion | flops 47185920 | bytes 21032960 | tf_op jit(solution)/shard_map/convert_element_type | solution.py:29
  341.2 4.8 %copy-done.1 = bf16[16,16,64,320]{3,0,2,1:T(8,128)(2,1)} copy-done((bf16[16,16,64,320]{3,0,2,1:T(8,128)(2,1)}, bf16[16,16,64,320]{3,0,2,1:T(8,128)(2,1)S(1)}, u32[]{:S(2)}) %copy-start.1) | copy-done | bytes 10485784
  346.1 1.4 collective-permute-start.8
  347.5 1.3 collective-permute-start.9
  348.8 0.5 collective-permute-done.8
  349.4 4.1 collective-permute-done.9
  353.5 57.4 %fusion.17 = bf16[16,16,64,320]{3,0,2,1:T(8,128)(2,1)} fusion(bf16[16,16,64,320]{3,0,2,1:T(8,128)(2,1)} %get-tuple-element.62, f32[320]{0:T(512)S(1)} %copy-done.12, bf16[16,1,64,320]{3,0,2,1:T(8,128)(2,1)S(1)} %collective-permute-done.9, bf16[16,16,64,320]{3,0,2,1:T(8,128)(2,1)} %copy-done.1, bf16[16,1,64,320]{3,0,2,1:T(8,128)(2,1)S(1)} %collective-permute-done.8, ...), kind=kOutput, calls=%fused_computation.25 | convolution fusion | flops 29951262720 | bytes 39175424 | tf_op jit(solution)/shard_map/conv_general_dilated | solution.py:12
  410.9 1.2 slice.174
  412.1 11.6 %collective-permute-start.10 = (bf16[16,1,64,320]{3,0,2,1:T(8,128)(2,1)S(1)}, bf16[16,1,64,320]{3,0,2,1:T(8,128)(2,1)S(1)}, u32[]{:S(2)}, u32[]{:S(2)}) collective-permute-start(bf16[16,1,64,320]{3,0,2,1:T(8,128)(2,1)S(1)} %slice.174), channel_id=1, source_target_pairs={{0,1},{1,2},{2,3},{4,5},{5,6},{6,7}} | collective-permute-start | bytes 1966088 | tf_op jit(solution)/shard_map/ppermute | solution.py:38
  423.8 8.5 %copy.45 = bf16[16,16,64,320]{3,2,1,0:T(8,128)(2,1)} copy(bf16[16,16,64,320]{3,0,2,1:T(8,128)(2,1)S(1)} %bitcast.95) | data formatting | bytes 20971520
  432.3 8.3 %copy.46 = bf16[16,16,64,320]{3,2,1,0:T(8,128)(2,1)} copy(bf16[16,16,64,320]{3,0,2,1:T(8,128)(2,1)S(1)} %bitcast.97) | data formatting | bytes 20971520
  440.7 11.9 %copy.47 = bf16[16,16,64,320]{3,2,1,0:T(8,128)(2,1)} copy(bf16[16,16,64,320]{3,0,2,1:T(8,128)(2,1)} %fusion.17) | data formatting | bytes 20971520
  452.6 13.5 %add_convert_fusion.5 = bf16[16,8,32,320]{3,0,2,1:T(8,128)(2,1)S(1)} fusion(f32[320]{0:T(512)S(1)} %convert_element_type.154, bf16[3,3,320,320]{3,2,1,0:T(8,128)(2,1)S(1)} %copy-done, bf16[16,16,64,320]{3,0,2,1:T(8,128)(2,1)S(1)} %bitcast.99, bf16[16,1,64,320]{3,0,2,1:T(8,128)(2,1)S(1)} %collective-permute-done.10), kind=kOutput, calls=%fused_computation.67 | convolution fusion | flops 7496007680 | bytes 15607040 | tf_op jit(solution)/shard_map/conv_general_dilated | solution.py:12
  466.1 2.4 copy.48
  (101 shorter events, 3.0 us)
Async XLA Ops:
  0.6 452.0 %copy-start = (bf16[3,3,320,320]{3,2,1,0:T(8,128)(2,1)S(1)}, bf16[3,3,320,320]{3,2,1,0:T(8,128)(2,1)}, u32[]{:S(2)}) copy-start(bf16[3,3,320,320]{3,2,1,0:T(8,128)(2,1)} %param.30) | copy-start | bytes 5529604
  2.7 6.1 %collective-permute-start = (bf16[16,1,64,4]{0,3,2,1:T(4,128)(2,1)S(1)}, bf16[16,1,64,4]{0,3,2,1:T(4,128)(2,1)S(1)}, u32[]{:S(2)}, u32[]{:S(2)}) collective-permute-start(bf16[16,1,64,4]{0,3,2,1:T(4,128)(2,1)S(1)} %get-tuple-element.58), channel_id=1, source_target_pairs={{0,1},{1,2},{2,3},{4,5},{5,6},{6,7}} | collective-permute-start | bytes 24584 | tf_op jit(solution)/shard_map/ppermute | solution.py:38
  5.5 5.2 %collective-permute-start.1 = (bf16[16,1,64,4]{0,3,2,1:T(4,128)(2,1)S(1)}, bf16[16,1,64,4]{0,3,2,1:T(4,128)(2,1)S(1)}, u32[]{:S(2)}, u32[]{:S(2)}) collective-permute-start(bf16[16,1,64,4]{0,3,2,1:T(4,128)(2,1)S(1)} %get-tuple-element.59), channel_id=1, source_target_pairs={{1,0},{2,1},{3,2},{5,4},{6,5},{7,6}} | collective-permute-start | bytes 24584 | tf_op jit(solution)/shard_map/ppermute | solution.py:41
  37.1 13.0 %copy-start.6 = (bf16[2,320]{1,0:T(2,128)(2,1)S(1)}, bf16[2,320]{1,0:T(2,128)(2,1)}, u32[]{:S(2)}) copy-start(bf16[2,320]{1,0:T(2,128)(2,1)} %param.23) | copy-start | bytes 3844
  37.1 13.6 %copy-start.7 = (bf16[2,320]{1,0:T(2,128)(2,1)S(1)}, bf16[2,320]{1,0:T(2,128)(2,1)}, u32[]{:S(2)}) copy-start(bf16[2,320]{1,0:T(2,128)(2,1)} %param.25) | copy-start | bytes 3844
  37.1 14.2 %copy-start.8 = (bf16[2,320]{1,0:T(2,128)(2,1)S(1)}, bf16[2,320]{1,0:T(2,128)(2,1)}, u32[]{:S(2)}) copy-start(bf16[2,320]{1,0:T(2,128)(2,1)} %param.27) | copy-start | bytes 3844
  37.2 14.2 %copy-start.9 = (bf16[2,320]{1,0:T(2,128)(2,1)S(1)}, bf16[2,320]{1,0:T(2,128)(2,1)}, u32[]{:S(2)}) copy-start(bf16[2,320]{1,0:T(2,128)(2,1)} %param.26) | copy-start | bytes 3844
  37.2 14.8 %copy-start.16 = (bf16[2,1280,320]{1,2,0:T(8,128)(2,1)S(1)}, bf16[2,1280,320]{1,2,0:T(8,128)(2,1)}, u32[]{:S(2)}) copy-start(bf16[2,1280,320]{1,2,0:T(8,128)(2,1)} %param.24) | copy-start | bytes 4915204
  37.2 14.8 %copy-start.18 = (bf16[16,1280]{1,0:T(8,128)(2,1)S(1)}, bf16[16,1280]{1,0:T(8,128)(2,1)}, u32[]{:S(2)}) copy-start(bf16[16,1280]{1,0:T(8,128)(2,1)} %param.17) | copy-start | bytes 122884
  47.4 4.9 %collective-permute-start.2 = (bf16[16,1,64,320]{3,0,2,1:T(8,128)(2,1)S(1)}, bf16[16,1,64,320]{3,0,2,1:T(8,128)(2,1)S(1)}, u32[]{:S(2)}, u32[]{:S(2)}) collective-permute-start(bf16[16,1,64,320]{3,0,2,1:T(8,128)(2,1)S(1)} %get-tuple-element.56), channel_id=1, source_target_pairs={{0,1},{1,2},{2,3},{4,5},{5,6},{6,7}} | collective-permute-start | bytes 1966088 | tf_op jit(solution)/shard_map/ppermute | solution.py:38
  48.8 5.9 %collective-permute-start.3 = (bf16[16,1,64,320]{3,0,2,1:T(8,128)(2,1)S(1)}, bf16[16,1,64,320]{3,0,2,1:T(8,128)(2,1)S(1)}, u32[]{:S(2)}, u32[]{:S(2)}) collective-permute-start(bf16[16,1,64,320]{3,0,2,1:T(8,128)(2,1)S(1)} %get-tuple-element.57), channel_id=1, source_target_pairs={{1,0},{2,1},{3,2},{5,4},{6,5},{7,6}} | collective-permute-start | bytes 1966088 | tf_op jit(solution)/shard_map/ppermute | solution.py:41
  134.4 13.3 %copy-start.10 = (bf16[2,320]{1,0:T(2,128)(2,1)S(1)}, bf16[2,320]{1,0:T(2,128)(2,1)}, u32[]{:S(2)}) copy-start(bf16[2,320]{1,0:T(2,128)(2,1)} %param.29) | copy-start | bytes 3844
  145.0 3.3 collective-permute-start.4
  146.4 5.9 %collective-permute-start.5 = (bf16[16,1,64,320]{3,0,2,1:T(8,128)(2,1)S(1)}, bf16[16,1,64,320]{3,0,2,1:T(8,128)(2,1)S(1)}, u32[]{:S(2)}, u32[]{:S(2)}) collective-permute-start(bf16[16,1,64,320]{3,0,2,1:T(8,128)(2,1)S(1)} %get-tuple-element.55), channel_id=1, source_target_pairs={{1,0},{2,1},{3,2},{5,4},{6,5},{7,6}} | collective-permute-start | bytes 1966088 | tf_op jit(solution)/shard_map/ppermute | solution.py:41
  152.3 81.7 %copy-start.2 = (f32[320]{0:T(512)S(1)}, f32[320]{0:T(512)}, u32[]{:S(2)}) copy-start(f32[320]{0:T(512)} %get-tuple-element.34) | copy-start | bytes 3844
  152.3 81.7 %copy-start.3 = (f32[320]{0:T(512)S(1)}, f32[320]{0:T(512)}, u32[]{:S(2)}) copy-start(f32[320]{0:T(512)} %get-tuple-element.65) | copy-start | bytes 3844
  234.0 13.0 %copy-start.13 = (f32[320]{0:T(512)S(1)}, f32[320]{0:T(512)}, u32[]{:S(2)}) copy-start(f32[320]{0:T(512)} %get-tuple-element.32) | copy-start | bytes 3844
  234.0 13.0 %copy-start.17 = (bf16[2,1280,320]{1,2,0:T(8,128)(2,1)S(1)}, bf16[2,1280,320]{1,2,0:T(8,128)(2,1)}, u32[]{:S(2)}) copy-start(bf16[2,1280,320]{1,2,0:T(8,128)(2,1)} %param.24) | copy-start | bytes 4915204
  234.0 13.0 %copy-start.19 = (bf16[16,1280]{1,0:T(8,128)(2,1)S(1)}, bf16[16,1280]{1,0:T(8,128)(2,1)}, u32[]{:S(2)}) copy-start(bf16[16,1280]{1,0:T(8,128)(2,1)} %param.17) | copy-start | bytes 122884
  234.0 17.6 %copy-start.11 = (f32[320]{0:T(512)S(1)}, f32[320]{0:T(512)}, u32[]{:S(2)}) copy-start(f32[320]{0:T(512)} %get-tuple-element.38) | copy-start | bytes 3844
  234.0 17.6 %copy-start.15 = (bf16[2,3,3,320,320]{4,3,2,1,0:T(8,128)(2,1)S(1)}, bf16[2,3,3,320,320]{4,3,2,1,0:T(8,128)(2,1)}, u32[]{:S(2)}) copy-start(bf16[2,3,3,320,320]{4,3,2,1,0:T(8,128)(2,1)} %param.22) | copy-start | bytes 11059204
  244.3 3.3 collective-permute-start.6
  245.7 5.9 %collective-permute-start.7 = (bf16[16,1,64,320]{3,0,2,1:T(8,128)(2,1)S(1)}, bf16[16,1,64,320]{3,0,2,1:T(8,128)(2,1)S(1)}, u32[]{:S(2)}, u32[]{:S(2)}) collective-permute-start(bf16[16,1,64,320]{3,0,2,1:T(8,128)(2,1)S(1)} %get-tuple-element.53), channel_id=1, source_target_pairs={{1,0},{2,1},{3,2},{5,4},{6,5},{7,6}} | collective-permute-start | bytes 1966088 | tf_op jit(solution)/shard_map/ppermute | solution.py:41
  251.6 78.3 %copy-start.4 = (f32[320]{0:T(512)S(1)}, f32[320]{0:T(512)}, u32[]{:S(2)}) copy-start(f32[320]{0:T(512)} %get-tuple-element.28) | copy-start | bytes 3844
  251.7 78.3 %copy-start.5 = (f32[320]{0:T(512)S(1)}, f32[320]{0:T(512)}, u32[]{:S(2)}) copy-start(f32[320]{0:T(512)} %get-tuple-element.67) | copy-start | bytes 3844
  330.0 23.4 %copy-start.12 = (f32[320]{0:T(512)S(1)}, f32[320]{0:T(512)}, u32[]{:S(2)}) copy-start(f32[320]{0:T(512)} %get-tuple-element.40) | copy-start | bytes 3844
  330.0 93.7 %slice-start = ((s8[12582912]{0:T(1024)(128)(4,1)}), s8[4194304]{0:T(1024)(128)(4,1)S(1)}, s32[]{:S(2)}) async-start(s8[12582912]{0:T(1024)(128)(4,1)} %bitcast.94), calls=%async_computation | async-start | bytes 8388608
  330.0 102.2 %slice-start.3 = ((s8[12582912]{0:T(1024)(128)(4,1)}), s8[4194304]{0:T(1024)(128)(4,1)S(1)}, s32[]{:S(2)}) async-start(s8[12582912]{0:T(1024)(128)(4,1)} %bitcast.96), calls=%async_computation.3 | async-start | bytes 8388608
  341.2 4.8 %copy-start.1 = (bf16[16,16,64,320]{3,0,2,1:T(8,128)(2,1)}, bf16[16,16,64,320]{3,0,2,1:T(8,128)(2,1)S(1)}, u32[]{:S(2)}) copy-start(bf16[16,16,64,320]{3,0,2,1:T(8,128)(2,1)S(1)} %multiply_convert_fusion) | copy-start | bytes 31457284
  346.1 3.3 collective-permute-start.8
  347.5 5.9 %collective-permute-start.9 = (bf16[16,1,64,320]{3,0,2,1:T(8,128)(2,1)S(1)}, bf16[16,1,64,320]{3,0,2,1:T(8,128)(2,1)S(1)}, u32[]{:S(2)}, u32[]{:S(2)}) collective-permute-start(bf16[16,1,64,320]{3,0,2,1:T(8,128)(2,1)S(1)} %get-tuple-element.51), channel_id=1, source_target_pairs={{1,0},{2,1},{3,2},{5,4},{6,5},{7,6}} | collective-permute-start | bytes 1966088 | tf_op jit(solution)/shard_map/ppermute | solution.py:41
  353.4 70.3 %copy-start.14 = (bf16[320]{0:T(512)(128)(2,1)S(1)}, bf16[320]{0:T(512)(128)(2,1)}, u32[]{:S(2)}) copy-start(bf16[320]{0:T(512)(128)(2,1)} %param.31) | copy-start | bytes 1924
  353.4 70.3 %slice-start.1 = ((s8[12582912]{0:T(1024)(128)(4,1)}), s8[4194304]{0:T(1024)(128)(4,1)S(1)}, s32[]{:S(2)}) async-start(s8[12582912]{0:T(1024)(128)(4,1)} %bitcast.94), calls=%async_computation.1 | async-start | bytes 8388608
  353.5 70.3 %slice-start.2 = ((s8[12582912]{0:T(1024)(128)(4,1)}), s8[4194304]{0:T(1024)(128)(4,1)S(1)}, s32[]{:S(2)}) async-start(s8[12582912]{0:T(1024)(128)(4,1)} %bitcast.94), calls=%async_computation.2 | async-start | bytes 8388608
  353.5 78.8 %slice-start.4 = ((s8[12582912]{0:T(1024)(128)(4,1)}), s8[4194304]{0:T(1024)(128)(4,1)S(1)}, s32[]{:S(2)}) async-start(s8[12582912]{0:T(1024)(128)(4,1)} %bitcast.96), calls=%async_computation.4 | async-start | bytes 8388608
  353.5 78.8 %slice-start.5 = ((s8[12582912]{0:T(1024)(128)(4,1)}), s8[4194304]{0:T(1024)(128)(4,1)S(1)}, s32[]{:S(2)}) async-start(s8[12582912]{0:T(1024)(128)(4,1)} %bitcast.96), calls=%async_computation.5 | async-start | bytes 8388608
  412.1 40.5 %collective-permute-start.10 = (bf16[16,1,64,320]{3,0,2,1:T(8,128)(2,1)S(1)}, bf16[16,1,64,320]{3,0,2,1:T(8,128)(2,1)S(1)}, u32[]{:S(2)}, u32[]{:S(2)}) collective-permute-start(bf16[16,1,64,320]{3,0,2,1:T(8,128)(2,1)S(1)} %slice.174), channel_id=1, source_target_pairs={{0,1},{1,2},{2,3},{4,5},{5,6},{6,7}} | collective-permute-start | bytes 1966088 | tf_op jit(solution)/shard_map/ppermute | solution.py:38
  432.3 20.3 %slice-start.6 = ((s8[12582912]{0:T(1024)(128)(4,1)}), s8[4194304]{0:T(1024)(128)(4,1)S(1)}, s32[]{:S(2)}) async-start(s8[12582912]{0:T(1024)(128)(4,1)} %bitcast.98), calls=%async_computation.6 | async-start | bytes 8388608
  432.3 20.3 %slice-start.7 = ((s8[12582912]{0:T(1024)(128)(4,1)}), s8[4194304]{0:T(1024)(128)(4,1)S(1)}, s32[]{:S(2)}) async-start(s8[12582912]{0:T(1024)(128)(4,1)} %bitcast.98), calls=%async_computation.7 | async-start | bytes 8388608
  440.7 12.0 %slice-start.8 = ((s8[12582912]{0:T(1024)(128)(4,1)}), s8[4194304]{0:T(1024)(128)(4,1)S(1)}, s32[]{:S(2)}) async-start(s8[12582912]{0:T(1024)(128)(4,1)} %bitcast.98), calls=%async_computation.8 | async-start | bytes 8388608
where the time goes:
time: 475 us; the launch traced here: 469 us
  matrix products  260 us (55%)
  blocking collectives  71.7 us (15%)
  other arithmetic  47.3 us (10%)
  local copies, waits for them, and re-layouts  44.4 us (9%)
  starting transfers between devices  26.5 us (6%)
  waiting for transfers between devices  17.2 us (4%)
    conv_general_dilated x6, matrix products, conv_valid_rows(): lax.conv_general_dilated(inputs, kernel, (stride, stride), ((0, 0), (1, 1...  259 us
    convert_element_type x4, other arithmetic, norm_silu(): jax.nn.silu(values * scale_bc[:, None, None, :] + offset_bc[:, None, None...  41.5 us
    psum x2, blocking collectives, band_program(): sums_all = lax.psum(group_sums(mixed_in), 'sp')  39.2 us
    unnamed x63, local copies, waits for them, and re-layouts  38.1 us
    psum x2, blocking collectives, band_program(): sums_all = lax.psum(group_sums(hidden_f32), 'sp')  32.5 us
    ppermute x6, starting transfers between devices, row_from_above(): return lax.ppermute(band_block[:, -1:], 'sp', to_next)  20 us
    ppermute x5, waiting for transfers between devices, row_from_below(): return lax.ppermute(band_block[:, :1], 'sp', to_prev)  16.5 us
  transfers between devices with their start and end apart: 11, of which 7 were waited for; matrix products, arithmetic and copies ran while one was open for 7% of the time, Pallas kernels for 0%

commit v1 on v0

v1 whole, which is shorter than its diff:
```python
import functools

import jax
import jax.numpy as jnp
from jax import lax
from jax.experimental import pallas as pl
from jax.experimental.pallas import tpu as pltpu
from jax.sharding import PartitionSpec as P

F32 = jnp.float32
BF16 = jnp.bfloat16
GROUPS = 32
EPS = 1e-5
CH = 320
LANES = ((0, 128), (128, 256), (256, 320))
TRANS_B = (((1,), (1,)), ((), ()))
VMEM_LIMIT = 60 * 1024 * 1024


def f32_dot(a, b):
    return jnp.dot(a, b, preferred_element_type=F32, precision=lax.Precision.HIGHEST)


def group_matrix(first, chan_major):
    shape = (CH, 128) if chan_major else (128, CH)
    chan = lax.broadcasted_iota(jnp.int32, shape, 0 if chan_major else 1)
    grp = lax.broadcasted_iota(jnp.int32, shape, 1 if chan_major else 0) - first
    size = CH // GROUPS
    hit = (chan >= grp * size) & (chan < grp * size + size) & (grp >= 0) & (grp < GROUPS)
    return hit.astype(F32)


def transpose_weights(w_ref, wt_ref):
    for dy in range(3):
        for dx in range(3):
            wt_ref[dy, :, dx * 256:(dx + 1) * 256] = w_ref[dy, dx, 0:256, :].T
        rest = [w_ref[dy, dx, 256:320, :] for dx in range(3)]
        rest.append(jnp.zeros((64, CH), BF16))
        wt_ref[dy, :, 768:1024] = jnp.concatenate(rest, axis=0).T


def column_masks(cols):
    pos = lax.broadcasted_iota(jnp.int32, (cols, 128), 0)
    return pos == 0, pos == cols - 1


def put_shifted(x_ref, row0, cols, tile, left, mid, right):
    rows = pl.ds(row0, cols)
    if tile < 2:
        for dx, part in enumerate((left, mid, right)):
            x_ref[rows, dx * 256 + tile * 128:dx * 256 + tile * 128 + 128] = part.astype(BF16)
    else:
        x_ref[rows, 768:896] = jnp.concatenate([left, mid], axis=-1).astype(BF16)
        x_ref[rows, 896:1024] = jnp.concatenate([right, jnp.zeros_like(right)], axis=-1).astype(BF16)


def norm_rows(x_ref, get_row, scale, offset, rows, top, bottom, first, last):
    cols = 64
    at_left, at_right = column_masks(cols)
    for r in rows:
        for tile, (lo, hi) in enumerate(LANES):
            y = get_row(r, lo, hi).astype(F32) * scale[:, lo:hi] + offset[:, lo:hi]
            v = y * jnp.tanh(y) + y
            if r == first:
                v = jnp.where(top, jnp.zeros_like(v), v)
            if r == last:
                v = jnp.where(bottom, jnp.zeros_like(v), v)
            left = jnp.where(at_left[:, :hi - lo], 0.0, pltpu.roll(v, 1, 0))
            right = jnp.where(at_right[:, :hi - lo], 0.0, pltpu.roll(v, cols - 1, 0))
            put_shifted(x_ref, r * cols, cols, tile, left, v, right)


def fold8(v):
    return v.reshape(v.shape[0] // 8, 8, v.shape[1]).sum(axis=0)


def stage_kernel(x_first, x_odd, x_even, halo_a, halo_b, stats_in, vecs, w_ref, *rest, emb_in, emb_out, residual, want_stats, samples, count):
    rest = list(rest)
    emb_in_ref = rest.pop(0) if emb_in else None
    emb_out_ref = rest.pop(0) if emb_out else None
    res_ref = rest.pop(0) if residual else None
    out_ref = rest.pop(0)
    stats_out = rest.pop(0) if want_stats else None
    wt_ref, xa, xb, acc, scale_ref, offset_ref, sum_ref, sq_ref = rest
    step = pl.program_id(0)
    sp = lax.axis_index("sp")
    top, bottom = sp == 0, sp == lax.axis_size("sp") - 1

    def normalize(dst, src, sample, rows):
        scale = scale_ref[pl.ds(sample, 1), :]
        offset = offset_ref[pl.ds(sample, 1), :]

        def get_row(r, lo, hi):
            if r == 0:
                return halo_a[sample, :, lo:hi]
            if r == 17:
                return halo_b[sample, :, lo:hi]
            return src[0, r - 1, :, lo:hi]

        norm_rows(dst, get_row, scale, offset, rows, top, bottom, 0, 17)

    @pl.when(step == 0)
    def _():
        transpose_weights(w_ref, wt_ref)
        total = stats_in[0]
        for d in range(1, stats_in.shape[0]):
            total = total + stats_in[d]
        total = total * (1.0 / count)
        mean = total
        var = pltpu.roll(total, 128 - GROUPS, 1) - mean * mean
        inv = lax.rsqrt(var + EPS)
        expand = group_matrix(0, False)
        lane = lax.broadcasted_iota(jnp.int32, inv.shape, 1)
        inv = jnp.where(lane < GROUPS, inv, 0.0)
        mean = jnp.where(lane < GROUPS, mean, 0.0)
        scale = f32_dot(inv, expand) * vecs[0:1, :]
        mean = f32_dot(mean, expand)
        if emb_in:
            mean = mean - emb_in_ref[...]
        offset = vecs[1:2, :] - mean * scale
        scale_ref[...] = scale * 0.5
        offset_ref[...] = offset * 0.5
        normalize(xa, x_first, 0, range(18))

    bias = vecs[2:3, :]
    for sub, (cur, nxt, src) in enumerate(((xa, xb, x_odd), (xb, xa, x_even))):
        sample = step * 2 + sub
        nxt_sample = jnp.minimum(sample + 1, samples - 1)
        for half in range(2):
            total = None
            for dy in range(3):
                part = lax.dot_general(wt_ref[dy], cur[pl.ds((8 * half + dy) * 64, 512), :], TRANS_B, preferred_element_type=F32)
                total = part if total is None else total + part
            acc[2 * sub + half] = total
        normalize(nxt, src, nxt_sample, range(18))
        tot = jnp.zeros((8, CH), F32)
        tot_sq = jnp.zeros((8, CH), F32)
        for pair in range(8):
            half, part = pair // 4, pair % 4
            t = acc[2 * sub + half, :, part * 128:(part + 1) * 128].T + bias
            u = t.astype(BF16)
            if residual:
                u = (res_ref[sub, 2 * pair:2 * pair + 2].reshape(128, CH).astype(F32) + u.astype(F32)).astype(BF16)
            out_ref[sub, 2 * pair:2 * pair + 2] = u.reshape(2, 64, CH)
            if want_stats:
                v = u.astype(F32)
                if emb_out:
                    v = v + emb_out_ref[pl.ds(sample, 1), :]
                tot = tot + fold8(v)
                tot_sq = tot_sq + fold8(v * v)
        if want_stats:
            sum_ref[pl.ds(sample, 1), :] = tot.sum(axis=0, keepdims=True)
            sq_ref[pl.ds(sample, 1), :] = tot_sq.sum(axis=0, keepdims=True)

    if want_stats:
        @pl.when(step == pl.num_programs(0) - 1)
        def _():
            stats_out[...] = f32_dot(sum_ref[...], group_matrix(0, True)) + f32_dot(sq_ref[...], group_matrix(GROUPS, True))


def once(shape):
    return pl.BlockSpec(shape, lambda g: (0,) * len(shape), pipeline_mode=pl.Buffered(1))


def conv_stage(x, halo_a, halo_b, stats_in, vecs, w, *, emb_in=None, emb_out=None, residual=None, want_stats=True):
    samples, rows, cols, chans = x.shape
    count = float(rows * stats_in.shape[0] * cols * (chans // GROUPS))
    one = (1, rows, cols, chans)
    two = (2, rows, cols, chans)
    args = [x, x, x, halo_a, halo_b, stats_in, vecs, w]
    specs = [
        once(one),
        pl.BlockSpec(one, lambda g: (2 * g + 1, 0, 0, 0)),
        pl.BlockSpec(one, lambda g: (jnp.minimum(2 * g + 2, samples - 1), 0, 0, 0)),
        once(halo_a.shape), once(halo_b.shape), once(stats_in.shape), once(vecs.shape), once(w.shape),
    ]
    for emb in (emb_in, emb_out):
        if emb is not None:
            args.append(emb)
            specs.append(once(emb.shape))
    if residual is not None:
        args.append(residual)
        specs.append(pl.BlockSpec(two, lambda g: (g, 0, 0, 0)))
    out_shape = [jax.ShapeDtypeStruct(x.shape, BF16)]
    out_specs = [pl.BlockSpec(two, lambda g: (g, 0, 0, 0))]
    if want_stats:
        out_shape.append(jax.ShapeDtypeStruct((samples, 128), F32))
        out_specs.append(pl.BlockSpec((samples, 128), lambda g: (0, 0)))
    body = functools.partial(stage_kernel, emb_in=emb_in is not None, emb_out=emb_out is not None, residual=residual is not None, want_stats=want_stats, samples=samples, count=count)
    return pl.pallas_call(
        body,
        grid=(samples // 2,),
        in_specs=specs,
        out_specs=out_specs,
        out_shape=out_shape,
        scratch_shapes=[
            pltpu.VMEM((3, CH, 1024), BF16),
            pltpu.VMEM((18 * 64, 1024), BF16),
            pltpu.VMEM((18 * 64, 1024), BF16),
            pltpu.VMEM((4, CH, 512), F32),
            pltpu.VMEM((samples, CH), F32),
            pltpu.VMEM((samples, CH), F32),
            pltpu.VMEM((samples, CH), F32),
            pltpu.VMEM((samples, CH), F32),
        ],
        compiler_params=pltpu.CompilerParams(vmem_limit_bytes=VMEM_LIMIT),
        name="conv_stage",
    )(*args)


def first_kernel(lat_ref, w_ref, vecs, out_ref, halo_a, halo_b, stats_out, patch, acc, sum_ref, sq_ref):
    step = pl.program_id(0)
    lane = lax.broadcasted_iota(jnp.int32, (4, 128), 1)
    col = lane & 63
    shifted = {}
    for r in range(20):
        row = lat_ref[0, r]
        both = jnp.concatenate([row, row], axis=-1)
        for dx in range(3):
            moved = both if dx == 1 else pltpu.roll(both, 1 if dx == 0 else 127, 1)
            if dx == 0:
                moved = jnp.where(col == 0, 0.0, moved)
            if dx == 2:
                moved = jnp.where(col == 63, 0.0, moved)
            shifted[r, dx] = moved
    for pair in range(9):
        parts = []
        for dy in range(3):
            for dx in range(3):
                parts.append(jnp.where(lane < 64, shifted[2 * pair + dy, dx], shifted[2 * pair + 1 + dy, dx]))
                parts.append(jnp.zeros((4, 128), F32))
        parts += [jnp.zeros((4, 128), F32)] * 2
        patch[:, pair * 128:(pair + 1) * 128] = jnp.concatenate(parts, axis=0).astype(BF16)
    acc[...] = jnp.dot(w_ref[...], patch[...], preferred_element_type=F32)
    bias = vecs[2:3, :]
    tot = jnp.zeros((8, CH), F32)
    tot_sq = jnp.zeros((8, CH), F32)
    for pair in range(9):
        u = (acc[:, pair * 128:(pair + 1) * 128].T + bias).astype(BF16)
        upper, lower = u[:64], u[64:]
        if pair == 0:
            halo_a[0] = upper
        else:
            out_ref[0, 2 * pair - 1] = upper
        if pair == 8:
            halo_b[0] = lower
        else:
            out_ref[0, 2 * pair] = lower
        v = u.astype(F32)
        if pair == 0:
            v = v[64:]
        if pair == 8:
            v = v[:64]
        tot = tot + fold8(v)
        tot_sq = tot_sq + fold8(v * v)
    sum_ref[pl.ds(step, 1), :] = tot.sum(axis=0, keepdims=True)
    sq_ref[pl.ds(step, 1), :] = tot_sq.sum(axis=0, keepdims=True)

    @pl.when(step == pl.num_programs(0) - 1)
    def _():
        stats_out[...] = f32_dot(sum_ref[...], group_matrix(0, True)) + f32_dot(sq_ref[...], group_matrix(GROUPS, True))


def first_conv(lat, w_in, vecs):
    samples = lat.shape[0]
    w = jnp.pad(w_in.reshape(9, 4, CH), ((0, 1), (0, 4), (0, 0))).reshape(80, CH).T
    return pl.pallas_call(
        first_kernel,
        grid=(samples,),
        in_specs=[pl.BlockSpec((1,) + lat.shape[1:], lambda s: (s, 0, 0, 0)), once(w.shape), once(vecs.shape)],
        out_specs=[
            pl.BlockSpec((1, 16, 64, CH), lambda s: (s, 0, 0, 0)),
            pl.BlockSpec((1, 64, CH), lambda s: (s, 0, 0)),
            pl.BlockSpec((1, 64, CH), lambda s: (s, 0, 0)),
            pl.BlockSpec((samples, 128), lambda s: (0, 0)),
        ],
        out_shape=[
            jax.ShapeDtypeStruct((samples, 16, 64, CH), BF16),
            jax.ShapeDtypeStruct((samples, 64, CH), BF16),
            jax.ShapeDtypeStruct((samples, 64, CH), BF16),
            jax.ShapeDtypeStruct((samples, 128), F32),
        ],
        scratch_shapes=[
            pltpu.VMEM((80, 18 * 64), BF16),
            pltpu.VMEM((CH, 18 * 64), F32),
            pltpu.VMEM((samples, CH), F32),
            pltpu.VMEM((samples, CH), F32),
        ],
        compiler_params=pltpu.CompilerParams(vmem_limit_bytes=VMEM_LIMIT),
        name="conv_in",
    )(lat, w, vecs)


def down_kernel(x_ref, halo_a, vecs, w_ref, out_ref, wt_ref, xe, xo, wide, acc):
    step = pl.program_id(0)
    top = lax.axis_index("sp") == 0
    at_left, _ = column_masks(32)

    @pl.when(step == 0)
    def _():
        transpose_weights(w_ref, wt_ref)

    bias = vecs[2:3, :]
    for sub in range(2):
        for r in range(17):
            dst, row0 = (xe, 32 * (r // 2)) if r % 2 == 0 else (xo, 32 * (r // 2))
            for tile, (lo, hi) in enumerate(LANES):
                v = halo_a[step * 2 + sub, :, lo:hi] if r == 0 else x_ref[sub, r - 1, :, lo:hi]
                v = v.astype(F32)
                if r == 0:
                    v = jnp.where(top, jnp.zeros_like(v), v)
                slot = (r * 3 + tile) % 8
                wide[slot, :, 0:hi - lo] = v
                even = wide[slot, pl.ds(0, 32, stride=2), 0:hi - lo]
                odd = wide[slot, pl.ds(1, 32, stride=2), 0:hi - lo]
                left = jnp.where(at_left[:, :hi - lo], 0.0, pltpu.roll(odd, 1, 0))
                put_shifted(dst.at[sub], row0, 32, tile, left, even, odd)
        total = None
        for dy, src in enumerate((xe.at[sub, pl.ds(0, 256)], xo.at[sub], xe.at[sub, pl.ds(32, 256)])):
            part = lax.dot_general(wt_ref[dy], src[...], TRANS_B, preferred_element_type=F32)
            total = part if total is None else total + part
        acc[sub] = total
        for part in range(2):
            u = (acc[sub, :, part * 128:(part + 1) * 128].T + bias).astype(BF16)
            out_ref[sub, 4 * part:4 * part + 4] = u.reshape(4, 32, CH)


def down_conv(x, halo_a, vecs, w):
    samples = x.shape[0]
    return pl.pallas_call(
        down_kernel,
        grid=(samples // 2,),
        in_specs=[pl.BlockSpec((2, 16, 64, CH), lambda g: (g, 0, 0, 0)), once(halo_a.shape), once(vecs.shape), once(w.shape)],
        out_specs=pl.BlockSpec((2, 8, 32, CH), lambda g: (g, 0, 0, 0)),
        out_shape=jax.ShapeDtypeStruct((samples, 8, 32, CH), BF16),
        scratch_shapes=[
            pltpu.VMEM((3, CH, 1024), BF16),
            pltpu.VMEM((2, 9 * 32, 1024), BF16),
            pltpu.VMEM((2, 8 * 32, 1024), BF16),
            pltpu.VMEM((8, 64, 128), F32),
            pltpu.VMEM((2, CH, 256), F32),
        ],
        compiler_params=pltpu.CompilerParams(vmem_limit_bytes=VMEM_LIMIT),
        name="down",
    )(x, halo_a, vecs, w)


def exchange_kernel(*refs, peers, stats, above, below):
    refs = list(refs)
    stats_ref = refs.pop(0) if stats else None
    x_ref = refs.pop(0) if above or below else None
    all_ref = refs.pop(0) if stats else None
    halo_a = refs.pop(0) if above else None
    halo_b = refs.pop(0) if below else None
    s_send, s_recv, h_send, h_recv = refs
    me = lax.axis_index("sp")
    barrier = pltpu.get_barrier_semaphore()
    for d in range(1, peers):
        pl.semaphore_signal(barrier, inc=1, device_id={"sp": lax.rem(me + d, peers)}, device_id_type=pl.DeviceIdType.MESH)
    pl.semaphore_wait(barrier, peers - 1)
    copies = []
    if stats:
        for d in range(1, peers):
            copy = pltpu.make_async_remote_copy(stats_ref, all_ref.at[me], s_send.at[d], s_recv.at[d], device_id={"sp": lax.rem(me + d, peers)}, device_id_type=pl.DeviceIdType.MESH)
            copy.start()
            copies.append(copy)
    last = x_ref.shape[1] - 1 if above or below else 0
    down_copy = up_copy = None
    if above:
        down_copy = pltpu.make_async_remote_copy(x_ref.at[:, last], halo_a, h_send.at[0], h_recv.at[0], device_id={"sp": lax.rem(me + 1, peers)}, device_id_type=pl.DeviceIdType.MESH)
        pl.when(me < peers - 1)(lambda: down_copy.start())
    if below:
        up_copy = pltpu.make_async_remote_copy(x_ref.at[:, 0], halo_b, h_send.at[1], h_recv.at[1], device_id={"sp": lax.rem(me + peers - 1, peers)}, device_id_type=pl.DeviceIdType.MESH)
        pl.when(me > 0)(lambda: up_copy.start())
    if stats:
        all_ref[me] = stats_ref[...]
    for copy in copies:
        copy.wait()
    if above:
        pl.when(me < peers - 1)(lambda: down_copy.wait_send())
        pl.when(me > 0)(lambda: down_copy.wait_recv())
    if below:
        pl.when(me > 0)(lambda: up_copy.wait_send())
        pl.when(me < peers - 1)(lambda: up_copy.wait_recv())


def exchange(peers, collective_id, stats=None, x=None, above=False, below=False):
    args, in_specs, out_shape, out_specs = [], [], [], []
    if stats is not None:
        args.append(stats)
        in_specs.append(pl.BlockSpec(memory_space=pltpu.VMEM))
        out_shape.append(jax.ShapeDtypeStruct((peers,) + stats.shape, F32))
        out_specs.append(pl.BlockSpec(memory_space=pltpu.VMEM))
    if x is not None:
        args.append(x)
        in_specs.append(pl.BlockSpec(memory_space=pl.ANY))
        for want in (above, below):
            if want:
                out_shape.append(jax.ShapeDtypeStruct((x.shape[0],) + x.shape[2:], x.dtype))
                out_specs.append(pl.BlockSpec(memory_space=pl.ANY))
    return pl.pallas_call(
        functools.partial(exchange_kernel, peers=peers, stats=stats is not None, above=above, below=below),
        in_specs=in_specs,
        out_specs=out_specs,
        out_shape=out_shape,
        scratch_shapes=[pltpu.SemaphoreType.DMA((peers,)), pltpu.SemaphoreType.DMA((peers,)), pltpu.SemaphoreType.DMA((2,)), pltpu.SemaphoreType.DMA((2,))],
        compiler_params=pltpu.CompilerParams(collective_id=collective_id, has_side_effects=True),
        name="exchange",
    )(*args)


def solution(mesh):
    peers = mesh.shape["sp"]
    to_next = [(d, d + 1) for d in range(peers - 1)]
    to_prev = [(d + 1, d) for d in range(peers - 1)]

    def vectors(*rows):
        rows = [r.astype(F32) for r in rows]
        rows += [jnp.zeros((CH,), F32)] * (8 - len(rows))
        return jnp.stack(rows)

    def band_program(latent, time_emb, w_in, b_in, gn1_scale, gn1_shift, conv1_w, conv1_b, temb_w, temb_b, gn2_scale, gn2_shift, conv2_w, conv2_b, down_w, down_b):
        emb_act = jax.nn.silu(time_emb.astype(F32)).astype(BF16)
        embs = [jnp.dot(emb_act, temb_w[i], preferred_element_type=F32) + temb_b[i].astype(F32) for i in range(2)]
        lat = latent.transpose(0, 1, 3, 2)
        above = lax.ppermute(lat[:, -2:], "sp", to_next)
        below = lax.ppermute(lat[:, :2], "sp", to_prev)
        lat = jnp.concatenate([above, lat, below], axis=1).astype(F32)
        zero = jnp.zeros((CH,), BF16)
        hidden, halo_a, halo_b, stats = first_conv(lat, w_in, vectors(zero, zero, b_in))
        outputs = [hidden]
        for i in range(2):
            vec1 = vectors(gn1_scale[i], gn1_shift[i], conv1_b[i])
            vec2 = vectors(gn2_scale[i], gn2_shift[i], conv2_b[i])
            if i == 0:
                (stats_all,) = exchange(peers, 0, stats=stats)
            else:
                stats_all, halo_a, halo_b = exchange(peers, 3 * i, stats=stats, x=hidden, above=True, below=True)
            branch, stats = conv_stage(hidden, halo_a, halo_b, stats_all, vec1, conv1_w[i], emb_out=embs[i])
            stats_all, halo_a, halo_b = exchange(peers, 3 * i + 1, stats=stats, x=branch, above=True, below=True)
            got = conv_stage(branch, halo_a, halo_b, stats_all, vec2, conv2_w[i], emb_in=embs[i], residual=hidden, want_stats=i == 0)
            hidden = got[0]
            stats = got[1] if i == 0 else None
            outputs.append(hidden)
        (halo_a,) = exchange(peers, 7, x=hidden, above=True)
        outputs.append(down_conv(hidden, halo_a, vectors(zero, zero, down_b), down_w))
        return tuple(outputs)

    band = P("dp", "sp", None, None)
    return jax.shard_map(band_program, mesh=mesh, in_specs=(band, P("dp", None)) + (P(),) * 14, out_specs=(band,) * 4, check_vma=False)
```

time: 475 us -> 328 us (0.69)
  the two profiles are of different devices: /device:TPU:0 before, /device:TPU:1 now
where the time goes in v1:
time: 328 us; the launch traced here: 327 us
  Pallas kernels  298 us (91%)
  local copies, waits for them, and re-layouts  12.9 us (4%)
  starting transfers between devices  6.43 us (2%)
  matrix products  4.35 us (1%)
  other arithmetic  4.08 us (1%)
    pallas_call x4, Pallas kernels, conv_stage(): pl.pallas_call(body, grid=(samples // 2,), in_specs=specs, out_specs=out_...  208 us
    pallas_call x5, Pallas kernels, exchange(): pl.pallas_call(functools.partial(exchange_kernel, peers=peers, stats=stat...  55.3 us
    pallas_call x1, Pallas kernels, down_conv(): pl.pallas_call(down_kernel, grid=(samples // 2,), in_specs=[pl.BlockSpec(...  18.8 us
    pallas_call x1, Pallas kernels, first_conv(): pl.pallas_call(first_kernel, grid=(samples,), in_specs=[pl.BlockSpec((1,)...  16.4 us
  transfers between devices with their start and end apart: 2, of which 0 were waited for; matrix products, arithmetic and copies ran while one was open for 6% of the time, Pallas kernels for 0%

profile of v1, /device:TPU:1, one launch (start us, length us, event | category | flops | bytes accessed | tf_op | source)
XLA Modules:
  0.0 326.8 jit_solution(955917880794014724)
XLA Ops:
  0.6 0.8 fusion.10
  1.4 4.5 %collective-permute-start = (bf16[16,2,4,64]{3,2,1,0:T(4,128)(2,1)S(1)}, bf16[16,2,4,64]{3,2,1,0:T(4,128)(2,1)S(1)}, u32[]{:S(2)}, u32[]{:S(2)}) collective-permute-start(bf16[16,2,4,64]{3,2,1,0:T(4,128)(2,1)S(1)} %get-tuple-element.48), channel_id=1, source_target_pairs={{0,1},{1,2},{2,3},{4,5},{5,6},{6,7}} | collective-permute-start | bytes 49160 | tf_op jit(solution)/shard_map/ppermute | solution.py:426
  6.0 1.9 collective-permute-start.1
  7.9 0.7 reshape.16
  8.6 0.7 reshape.19
  9.3 0.8 slice_convert_fusion.5
  10.0 0.8 slice_convert_fusion.2
  10.8 0.8 convert_reduce_fusion
  11.5 2.1 convolution_add_fusion.rest_0_
  13.7 0.0 slice-start
  13.7 2.2 convolution_add_fusion.1.rest_0_
  15.9 0.0 slice-start.1
  15.9 4.9 %slice_bitcast_fusion.1 = (bf16[3,3,320,320]{3,2,1,0:T(8,128)(2,1)}, bf16[3,3,320,320]{3,2,1,0:T(8,128)(2,1)}) fusion(bf16[2,3,3,320,320]{4,3,2,1,0:T(8,128)(2,1)} %param.22), kind=kLoop, calls=%fused_computation.1 | loop fusion | bytes 7372800 | tf_op jit(solution)/shard_map/squeeze | solution.py:439
  20.8 0.0 slice-done
  20.8 0.0 slice-done.1
  20.8 0.0 copy-start.2
  20.8 0.0 copy-start.3
  20.8 0.0 copy-start.4
  20.8 0.0 copy-start.5
  20.8 0.0 copy-start.1
  20.8 0.0 copy-start
  20.8 2.5 slice_bitcast_fusion
  23.4 0.0 copy-done.2
  23.4 0.0 copy-done.3
  23.4 0.0 copy-done.4
  23.4 0.0 copy-done.5
  23.5 0.7 pad_maximum_fusion
  24.1 0.0 copy-done.1
  24.2 0.8 copy.21
  24.9 0.6 stack.48.vecs
  25.5 0.6 stack.47.vecs
  26.2 0.6 stack.46.vecs
  26.8 0.6 stack.45.vecs
  27.4 0.0 collective-permute-done
  27.4 0.0 collective-permute-done.1
  27.4 0.0 copy-done
  27.4 1.1 maximum_convert_fusion.lat_ref
  28.5 16.4 %conv_in.1 = (bf16[16,16,64,320]{3,2,1,0:T(8,128)(2,1)}, bf16[16,64,320]{2,1,0:T(8,128)(2,1)}, bf16[16,64,320]{2,1,0:T(8,128)(2,1)}, f32[16,128]{1,0:T(8,128)}) custom-call(f32[16,20,4,64]{3,2,1,0:T(4,128)} %maximum_convert_fusion.lat_ref, bf16[320,80]{1,0:T(8,128)(2,1)} %bitcast.23, f32[8,320]{1,0:T(8,128)} %get-tuple-element.51.vecs), custom_call_target="tpu_custom_call" | custom-call | tf_op jit(solution)/shard_map/conv_in/pallas_call | solution.py:267
  44.9 4.8 %exchange.5.stats_in = f32[4,16,128]{2,1,0:T(8,128)} custom-call(f32[16,128]{1,0:T(8,128)} %get-tuple-element.26.refs_0_), custom_call_target="tpu_custom_call" | custom-call | tf_op jit(solution)/shard_map/exchange/pallas_call | solution.py:401
  49.7 51.4 %conv_stage.4 = (bf16[16,16,64,320]{3,2,1,0:T(8,128)(2,1)}, f32[16,128]{1,0:T(8,128)}) custom-call(bf16[16,16,64,320]{3,2,1,0:T(8,128)(2,1)} %get-tuple-element.19.x_first.x_odd.x_even.rest_1_, bf16[16,16,64,320]{3,2,1,0:T(8,128)(2,1)} %get-tuple-element.19.x_first.x_odd.x_even.rest_1_, ...), custom_call_target="tpu_custom_call" | custom-call | tf_op jit(solution)/shard_map/conv_stage/pallas_call | solution.py:190
  101.1 13.4 %exchange.6 = (f32[4,16,128]{2,1,0:T(8,128)}, bf16[16,64,320]{2,1,0:T(8,128)(2,1)}, bf16[16,64,320]{2,1,0:T(8,128)(2,1)}) custom-call(f32[16,128]{1,0:T(8,128)} %get-tuple-element.28.refs_0_, bf16[16,16,64,320]{3,2,1,0:T(8,128)(2,1)} %get-tuple-element.27.refs_1_.x_first.x_odd.x_even), custom_call_target="tpu_custom_call" | custom-call | tf_op jit(solution)/shard_map/exchange/pallas_call | solution.py:401
  114.5 53.7 %conv_stage.5 = (bf16[16,16,64,320]{3,2,1,0:T(8,128)(2,1)}, f32[16,128]{1,0:T(8,128)}) custom-call(bf16[16,16,64,320]{3,2,1,0:T(8,128)(2,1)} %get-tuple-element.27.refs_1_.x_first.x_odd.x_even, bf16[16,16,64,320]{3,2,1,0:T(8,128)(2,1)} %get-tuple-element.27.refs_1_.x_first.x_odd.x_even, ...), custom_call_target="tpu_custom_call" | custom-call | tf_op jit(solution)/shard_map/conv_stage/pallas_call | solution.py:190
  168.2 13.1 %exchange.7 = (f32[4,16,128]{2,1,0:T(8,128)}, bf16[16,64,320]{2,1,0:T(8,128)(2,1)}, bf16[16,64,320]{2,1,0:T(8,128)(2,1)}) custom-call(f32[16,128]{1,0:T(8,128)} %get-tuple-element.33.refs_0_, bf16[16,16,64,320]{3,2,1,0:T(8,128)(2,1)} %get-tuple-element.20.refs_1_.x_first.x_odd.x_even.rest_1_), custom_call_target="tpu_custom_call" | custom-call | tf_op jit(solution)/shard_map/exchange/pallas_call | solution.py:401
  181.2 51.7 %conv_stage.6 = (bf16[16,16,64,320]{3,2,1,0:T(8,128)(2,1)}, f32[16,128]{1,0:T(8,128)}) custom-call(bf16[16,16,64,320]{3,2,1,0:T(8,128)(2,1)} %get-tuple-element.20.refs_1_.x_first.x_odd.x_even.rest_1_, bf16[16,16,64,320]{3,2,1,0:T(8,128)(2,1)} %get-tuple-element.20.refs_1_.x_first.x_odd.x_even.rest_1_, ...), custom_call_target="tpu_custom_call" | custom-call | tf_op jit(solution)/shard_map/conv_stage/pallas_call | solution.py:190
  232.9 13.2 %exchange.8 = (f32[4,16,128]{2,1,0:T(8,128)}, bf16[16,64,320]{2,1,0:T(8,128)(2,1)}, bf16[16,64,320]{2,1,0:T(8,128)(2,1)}) custom-call(f32[16,128]{1,0:T(8,128)} %get-tuple-element.38.refs_0_, bf16[16,16,64,320]{3,2,1,0:T(8,128)(2,1)} %get-tuple-element.37.refs_1_.x_first.x_odd.x_even), custom_call_target="tpu_custom_call" | custom-call | tf_op jit(solution)/shard_map/exchange/pallas_call | solution.py:401
  246.1 50.9 %conv_stage.7.refs_0_.x_ref = bf16[16,16,64,320]{3,2,1,0:T(8,128)(2,1)} custom-call(bf16[16,16,64,320]{3,2,1,0:T(8,128)(2,1)} %get-tuple-element.37.refs_1_.x_first.x_odd.x_even, bf16[16,16,64,320]{3,2,1,0:T(8,128)(2,1)} %get-tuple-element.37.refs_1_.x_first.x_odd.x_even, bf16[16,16,64,320]{3,2,1,0:T(8,128)(2,1)} %get-tuple-element.37.refs_1_.x_first.x_odd.x_even, ...), custom_call_target="tpu_custom_call" | custom-call | tf_op jit(solution)/shard_map/conv_stage/pallas_call | solution.py:190
  297.0 10.9 %exchange.9.halo_a = bf16[16,64,320]{2,1,0:T(8,128)(2,1)} custom-call(bf16[16,16,64,320]{3,2,1,0:T(8,128)(2,1)} %conv_stage.7.refs_0_.x_ref), custom_call_target="tpu_custom_call" | custom-call | tf_op jit(solution)/shard_map/exchange/pallas_call | solution.py:401
  308.0 18.8 %down.1 = bf16[16,8,32,320]{3,2,1,0:T(8,128)(2,1)} custom-call(bf16[16,16,64,320]{3,2,1,0:T(8,128)(2,1)} %conv_stage.7.refs_0_.x_ref, bf16[16,64,320]{2,1,0:T(8,128)(2,1)} %exchange.9.halo_a, f32[8,320]{1,0:T(8,128)} %get-tuple-element.50.vecs, bf16[3,3,320,320]{3,2,1,0:T(8,128)(2,1)} %w_ref.1), custom_call_target="tpu_custom_call" | custom-call | tf_op jit(solution)/shard_map/down/pallas_call | solution.py:330
  (8 shorter events, 0.0 us)
Async XLA Ops:
  1.4 25.9 %collective-permute-start = (bf16[16,2,4,64]{3,2,1,0:T(4,128)(2,1)S(1)}, bf16[16,2,4,64]{3,2,1,0:T(4,128)(2,1)S(1)}, u32[]{:S(2)}, u32[]{:S(2)}) collective-permute-start(bf16[16,2,4,64]{3,2,1,0:T(4,128)(2,1)S(1)} %get-tuple-element.48), channel_id=1, source_target_pairs={{0,1},{1,2},{2,3},{4,5},{5,6},{6,7}} | collective-permute-start | bytes 49160 | tf_op jit(solution)/shard_map/ppermute | solution.py:426
  6.0 21.4 %collective-permute-start.1 = (bf16[16,2,4,64]{3,2,1,0:T(4,128)(2,1)S(1)}, bf16[16,2,4,64]{3,2,1,0:T(4,128)(2,1)S(1)}, u32[]{:S(2)}, u32[]{:S(2)}) collective-permute-start(bf16[16,2,4,64]{3,2,1,0:T(4,128)(2,1)S(1)} %get-tuple-element.49), channel_id=1, source_target_pairs={{1,0},{2,1},{3,2},{5,4},{6,5},{7,6}} | collective-permute-start | bytes 49160 | tf_op jit(solution)/shard_map/ppermute | solution.py:427
  13.7 7.1 %slice-start = ((s8[4423680]{0:T(1024)(128)(4,1)}), s8[4194304]{0:T(1024)(128)(4,1)S(1)}, s32[]{:S(2)}) async-start(s8[4423680]{0:T(1024)(128)(4,1)} %bitcast.19), calls=%async_computation | async-start | bytes 8388608
  15.9 4.9 %slice-start.1 = ((s8[4423680]{0:T(1024)(128)(4,1)}), s8[229376]{0:T(1024)(128)(4,1)S(1)}, s32[]{:S(2)}) async-start(s8[4423680]{0:T(1024)(128)(4,1)} %bitcast.19), calls=%async_computation.1 | async-start | bytes 458752
  20.8 2.6 copy-start.2
  20.8 2.6 copy-start.3
  20.8 2.6 copy-start.4
  20.8 2.6 copy-start.5
  20.8 3.3 %copy-start.1 = (bf16[3,3,4,320]{3,2,1,0:T(4,128)(2,1)S(1)}, bf16[3,3,4,320]{3,2,1,0:T(4,128)(2,1)}, u32[]{:S(2)}) copy-start(bf16[3,3,4,320]{3,2,1,0:T(4,128)(2,1)} %param.18) | copy-start | bytes 69124
  20.8 6.6 %copy-start = (bf16[16,16,64,4]{2,3,1,0:T(4,128)(2,1)S(1)}, bf16[16,16,64,4]{2,3,1,0:T(4,128)(2,1)}, u32[]{:S(2)}) copy-start(bf16[16,16,64,4]{2,3,1,0:T(4,128)(2,1)} %param.16) | copy-start | bytes 393220

commit v2 on v0

v2 whole, which is shorter than its diff:
```python
import functools

import jax
import jax.numpy as jnp
from jax import lax
from jax.experimental import pallas as pl
from jax.experimental.pallas import tpu as pltpu
from jax.sharding import PartitionSpec as P

F32 = jnp.float32
BF16 = jnp.bfloat16
GROUPS = 32
EPS = 1e-5
LANE = 128
COLS = 64
FULL = 256
DEEP = 1024
ROWS = 16
CH = 320
WIDE = ((0, FULL), (FULL, 320))
TRANS_B = (((1,), (1,)), ((), ()))
VMEM_LIMIT = 60 * DEEP * DEEP


def f32_dot(a, b):
    return jnp.dot(a, b, preferred_element_type=F32, precision=lax.Precision.HIGHEST)


def group_matrix(first, chan_major):
    shape = (CH, LANE) if chan_major else (LANE, CH)
    chan = lax.broadcasted_iota(jnp.int32, shape, 0 if chan_major else 1)
    grp = lax.broadcasted_iota(jnp.int32, shape, 1 if chan_major else 0) - first
    size = CH // GROUPS
    hit = (chan >= grp * size) & (chan < grp * size + size) & (grp >= 0) & (grp < GROUPS)
    return hit.astype(F32)


def transpose_weights(w_ref, wt_ref):
    for dy in range(3):
        for dx in range(3):
            wt_ref[dy, :, dx * FULL:(dx + 1) * FULL] = w_ref[0, dy, dx, 0:FULL, :].T
        rest = [w_ref[0, dy, dx, FULL:320, :] for dx in range(3)]
        rest.append(jnp.zeros((COLS, CH), BF16))
        wt_ref[dy, :, 768:DEEP] = jnp.concatenate(rest, axis=0).T


def put_shifted(x_ref, row0, cols, tile, left, mid, right):
    rows = pl.ds(row0, cols)
    if tile == 0:
        for dx, part in enumerate((left, mid, right)):
            x_ref[rows, dx * FULL:dx * FULL + FULL] = part.astype(BF16)
    else:
        x_ref[rows, 768:DEEP] = jnp.concatenate([left, mid, right, jnp.zeros_like(right)], axis=-1).astype(BF16)


def norm_rows(x_ref, get_row, scale, offset, rows, top, bottom, first, last):
    cols = COLS
    for r in rows:
        for tile, (lo, hi) in enumerate(WIDE):
            y = get_row(r, lo, hi).astype(F32) * scale[:, lo:hi] + offset[:, lo:hi]
            v = y * jnp.tanh(y) + y
            if r == first:
                v = jnp.where(top, jnp.zeros_like(v), v)
            if r == last:
                v = jnp.where(bottom, jnp.zeros_like(v), v)
            padded = jnp.concatenate([v, jnp.zeros((8, hi - lo), F32)], axis=0)
            left = pltpu.roll(padded, 1, 0)[:cols]
            right = pltpu.roll(padded, cols + 7, 0)[:cols]
            put_shifted(x_ref, r * cols, cols, tile, left, v, right)


def fold8(v):
    return v.reshape(v.shape[0] // 8, 8, v.shape[1]).sum(axis=0)


def row_vector(ref, layer):
    return ref[...].astype(F32)[layer:layer + 1, :]


def remote(src, dst, send, recv, peer):
    return pltpu.make_async_remote_copy(src, dst, send, recv, device_id={"sp": peer}, device_id_type=pl.DeviceIdType.MESH)


def greet(me, peers):
    barrier = pltpu.get_barrier_semaphore()
    for d in range(1, peers):
        pl.semaphore_signal(barrier, inc=1, device_id={"sp": lax.rem(me + d, peers)}, device_id_type=pl.DeviceIdType.MESH)
    pl.semaphore_wait(barrier, peers - 1)


def to_all(src, slots, send, recv, me, peers):
    return [remote(src, slots.at[me], send.at[d], recv.at[d], lax.rem(me + d, peers)) for d in range(1, peers)]


class RowSend:
    def __init__(self, src, dst, send, recv, me, peers, step):
        self.copy = remote(src, dst, send, recv, lax.rem(me + peers + step, peers))
        self.sends = me < peers - 1 if step == 1 else me > 0
        self.receives = me > 0 if step == 1 else me < peers - 1

    def start(self):
        pl.when(self.sends)(lambda: self.copy.start())

    def wait_send(self):
        pl.when(self.sends)(lambda: self.copy.wait_send())

    def wait_recv(self):
        pl.when(self.receives)(lambda: self.copy.wait_recv())


HALO_GROUPS = ((0, 1), (1, 2), (3, 4), (7, 9))
HALO_STEPS = (None, 0, 1, 3)


def stage_kernel(*refs, layer, talk, halo_in, emb_in, emb_out, residual, want_stats, samples, count, peers):
    refs = list(refs)

    def take(wanted=True):
        return refs.pop(0) if wanted else None

    x_first, x_odd, x_even = take(), take(), take()
    halo_a, halo_b = take(not halo_in), take(not halo_in)
    x_any = take(halo_in)
    stats_in, gain_ref, shift_ref, bias_ref, w_ref = take(), take(), take(), take(), take()
    emb_in_ref, emb_out_ref, res_ref = take(emb_in), take(emb_out), take(residual)
    out_ref = take()
    stats_out = take(want_stats)
    out_a, out_b = take(talk), take(talk)
    wt_ref, xa, xb, scale_ref, offset_ref, sum_ref, sq_ref = (take() for _ in range(7))
    in_all, tx, out_all, edge, a_send, a_recv, b_send, b_recv, o_send, o_recv = (take(talk) for _ in range(10))
    if halo_in:
        halo_a, halo_b, i_send, i_recv = (take() for _ in range(4))
    step = pl.program_id(0)
    last_step = samples // 2 - 1
    me = lax.axis_index("sp")
    top, bottom = me == 0, me == peers - 1

    def normalize(dst, src, sample):
        scale = scale_ref[pl.ds(sample, 1), :]
        offset = offset_ref[pl.ds(sample, 1), :]

        def get_row(r, lo, hi):
            if r == 0:
                return halo_a[sample, :, lo:hi]
            if r == 17:
                return halo_b[sample, :, lo:hi]
            return src[0, r - 1, :, lo:hi]

        norm_rows(dst, get_row, scale, offset, range(18), top, bottom, 0, 17)

    def halo_group(i):
        first, size = HALO_GROUPS[i]
        part = pl.ds(first, size)
        return (
            RowSend(x_any.at[part, 15], halo_a.at[part], i_send.at[0, i], i_recv.at[0, i], me, peers, 1),
            RowSend(x_any.at[part, 0], halo_b.at[part], i_send.at[1, i], i_recv.at[1, i], me, peers, -1),
        )

    def edge_rows(pair):
        part = pl.ds(2 * pair, 2)
        return (
            RowSend(edge.at[part, 1], out_a.at[part], o_send.at[0, pair], o_recv.at[0, pair], me, peers, 1),
            RowSend(edge.at[part, 0], out_b.at[part], o_send.at[1, pair], o_recv.at[1, pair], me, peers, -1),
        )

    @pl.when(step == 0)
    def _():
        if talk:
            greet(me, peers)
            copies = to_all(stats_in, in_all, a_send, a_recv, me, peers)
            for copy in copies:
                copy.start()
            if halo_in:
                for i in range(len(HALO_GROUPS)):
                    for row in halo_group(i):
                        row.start()
            in_all[me] = stats_in[...]
        transpose_weights(w_ref, wt_ref)
        if talk:
            for copy in copies:
                copy.wait()
        bands = in_all if talk else stats_in
        total = bands[0]
        for d in range(1, peers):
            total = total + bands[d]
        total = total * (1.0 / count)
        var = pltpu.roll(total, LANE - GROUPS, 1) - total * total
        lane = lax.broadcasted_iota(jnp.int32, total.shape, 1)
        inv = jnp.where(lane < GROUPS, lax.rsqrt(var + EPS), 0.0)
        mean = jnp.where(lane < GROUPS, total, 0.0)
        expand = group_matrix(0, False)
        scale = f32_dot(inv, expand) * row_vector(gain_ref, layer)
        mean = f32_dot(mean, expand)
        if emb_in:
            mean = mean - emb_in_ref[0]
        offset = row_vector(shift_ref, layer) - mean * scale
        scale_ref[...] = scale * 0.5
        offset_ref[...] = offset * 0.5
        if halo_in:
            for row in halo_group(0):
                row.wait_recv()
        normalize(xa, x_first, 0)

    if halo_in:
        for i in range(1, len(HALO_GROUPS)):
            @pl.when(step == HALO_STEPS[i])
            def _():
                for row in halo_group(i):
                    row.wait_recv()
    if talk:
        @pl.when(step > 0)
        def _():
            for row in edge_rows(step - 1):
                row.start()

    bias = row_vector(bias_ref, layer)
    for sub, (cur, nxt, src) in enumerate(((xa, xb, x_odd), (xb, xa, x_even))):
        sample = step * 2 + sub
        nxt_sample = jnp.minimum(sample + 1, samples - 1)
        totals = []
        for half in range(2):
            total = None
            for dy in range(3):
                part = lax.dot_general(wt_ref[dy], cur[pl.ds((8 * half + dy) * COLS, 512), :], TRANS_B, preferred_element_type=F32)
                total = part if total is None else total + part
            totals.append(total)
        normalize(nxt, src, nxt_sample)
        tot = jnp.zeros((8, CH), F32)
        tot_sq = jnp.zeros((8, CH), F32)
        for pair in range(8):
            half, part = pair // 4, pair % 4
            u = (totals[half][:, part * LANE:(part + 1) * LANE].T + bias).astype(BF16)
            if residual:
                u = (res_ref[sub, 2 * pair:2 * pair + 2].reshape(LANE, CH).astype(F32) + u.astype(F32)).astype(BF16)
            out_ref[sub, 2 * pair:2 * pair + 2] = u.reshape(2, COLS, CH)
            if talk and pair == 0:
                edge[sample, 0] = u[:COLS]
            if talk and pair == 7:
                edge[sample, 1] = u[COLS:]
            if want_stats:
                v = u.astype(F32)
                if emb_out:
                    v = v + emb_out_ref[0, pl.ds(sample, 1), :]
                tot = tot + fold8(v)
                tot_sq = tot_sq + fold8(v * v)
        if want_stats:
            sum_ref[pl.ds(sample, 1), :] = tot.sum(axis=0, keepdims=True)
            sq_ref[pl.ds(sample, 1), :] = tot_sq.sum(axis=0, keepdims=True)

    if want_stats:
        @pl.when(step == last_step)
        def _():
            sums = group_sums(sum_ref, sq_ref)
            if not talk:
                stats_out[...] = sums
                return
            tx[...] = sums
            for row in edge_rows(last_step):
                row.start()
            out_all[me] = sums
            copies = to_all(tx, out_all, b_send, b_recv, me, peers)
            for copy in copies:
                copy.start()
            if halo_in:
                for i in range(len(HALO_GROUPS)):
                    for row in halo_group(i):
                        row.wait_send()
            for pair in range(samples // 2):
                for row in edge_rows(pair):
                    row.wait_send()
                    row.wait_recv()
            for copy in copies:
                copy.wait()
            stats_out[...] = out_all[...]


def group_sums(sum_ref, sq_ref):
    return f32_dot(sum_ref[...], group_matrix(0, True)) + f32_dot(sq_ref[...], group_matrix(GROUPS, True))


def once(shape):
    return pl.BlockSpec(shape, lambda g: (0,) * len(shape), pipeline_mode=pl.Buffered(1))


def layer_of(shape, layer):
    return pl.BlockSpec((1,) + shape[1:], lambda g: (layer,) + (0,) * (len(shape) - 1), pipeline_mode=pl.Buffered(1))


def conv_stage(x, halos, stats_in, gain, shift, bias, w, layer, peers, *, talk=None, emb_in=None, emb_out=None, residual=None, want_stats=True):
    samples, rows, cols, chans = x.shape
    count = float(rows * peers * cols * (chans // GROUPS))
    one = (1, rows, cols, chans)
    two = (2, rows, cols, chans)
    args = [x, x, x]
    specs = [
        once(one),
        pl.BlockSpec(one, lambda g: (2 * g + 1, 0, 0, 0)),
        pl.BlockSpec(one, lambda g: (jnp.minimum(2 * g + 2, samples - 1), 0, 0, 0)),
    ]
    halo_in = halos is None
    if halo_in:
        args.append(x)
        specs.append(pl.BlockSpec(memory_space=pl.ANY))
    else:
        args += list(halos)
        specs += [once(h.shape) for h in halos]
    args += [stats_in, gain, shift, bias, w]
    specs += [once(stats_in.shape), once(gain.shape), once(shift.shape), once(bias.shape), layer_of(w.shape, layer)]
    for emb in (emb_in, emb_out):
        if emb is not None:
            args.append(emb)
            specs.append(layer_of(emb.shape, layer))
    if residual is not None:
        args.append(residual)
        specs.append(pl.BlockSpec(two, lambda g: (g, 0, 0, 0)))
    out_shape = [jax.ShapeDtypeStruct(x.shape, BF16)]
    out_specs = [pl.BlockSpec(two, lambda g: (g, 0, 0, 0))]
    scratch = [
        pltpu.VMEM((3, CH, DEEP), BF16),
        pltpu.VMEM((18 * COLS, DEEP), BF16),
        pltpu.VMEM((18 * COLS, DEEP), BF16),
    ] + [pltpu.VMEM((samples, CH), F32)] * 4
    if want_stats:
        shape = (peers, samples, LANE) if talk is not None else (samples, LANE)
        out_shape.append(jax.ShapeDtypeStruct(shape, F32))
        out_specs.append(pl.BlockSpec(shape, lambda g: (0,) * len(shape)))
    if talk is not None:
        out_shape += [jax.ShapeDtypeStruct((samples, cols, chans), BF16)] * 2
        out_specs += [pl.BlockSpec(memory_space=pl.ANY)] * 2
        scratch += [
            pltpu.VMEM((peers, samples, LANE), F32),
            pltpu.VMEM((samples, LANE), F32),
            pltpu.VMEM((peers, samples, LANE), F32),
            pltpu.VMEM((samples, 2, cols, chans), BF16),
        ] + [pltpu.SemaphoreType.DMA((peers,))] * 4 + [pltpu.SemaphoreType.DMA((2, samples // 2))] * 2
    if halo_in:
        scratch += [pltpu.VMEM((samples, cols, chans), BF16)] * 2 + [pltpu.SemaphoreType.DMA((2, len(HALO_GROUPS)))] * 2
    body = functools.partial(stage_kernel, layer=layer, talk=talk is not None, halo_in=halo_in, emb_in=emb_in is not None, emb_out=emb_out is not None, residual=residual is not None, want_stats=want_stats, samples=samples, count=count, peers=peers)
    extra = {} if talk is None else {"collective_id": talk, "has_side_effects": True}
    return pl.pallas_call(
        body,
        grid=(samples // 2,),
        in_specs=specs,
        out_specs=out_specs,
        out_shape=out_shape,
        scratch_shapes=scratch,
        compiler_params=pltpu.CompilerParams(vmem_limit_bytes=VMEM_LIMIT, **extra),
        name="conv_stage_%d_%d" % (layer, 1 if talk is not None else 2),
    )(*args)


def first_kernel(lat_ref, halo_lat_a, halo_lat_b, w_ref, b_ref, time_ref, tw_ref, tb_ref, out_ref, halo_a, halo_b, stats_out, emb_ref, wt_ref, patch, sum_ref, sq_ref, *, peers, samples):
    step = pl.program_id(0)
    me = lax.axis_index("sp")

    @pl.when(step == 0)
    def _():
        parts = []
        for tap in range(9):
            parts.append(w_ref[tap // 3, tap % 3].astype(F32))
            parts.append(jnp.zeros((4, CH), F32))
        parts.append(jnp.zeros((LANE - 72, CH), F32))
        wt_ref[...] = jnp.concatenate(parts, axis=0).T.astype(BF16)[:, 0:80]
        time = time_ref[...].astype(F32)
        act = jax.nn.silu(time).astype(BF16)
        for i in range(2):
            emb = lax.dot_general(act, tw_ref[i], TRANS_B, preferred_element_type=F32)
            emb_ref[i] = emb + row_vector(tb_ref, i)

    lane = lax.broadcasted_iota(jnp.int32, (4, LANE), 1)
    col = lane & 63
    bias = b_ref[...].astype(F32).reshape(1, CH)
    zero4 = jnp.zeros((4, LANE), F32)
    for sub in range(2):
        sample = 2 * step + sub
        shifted = {}
        for r in range(20):
            if r < 2:
                row = halo_lat_a[sample, r].astype(F32)
                row = jnp.where(me == 0, jnp.zeros_like(row), row)
            elif r > 17:
                row = halo_lat_b[sample, r - 18].astype(F32)
                row = jnp.where(me == peers - 1, jnp.zeros_like(row), row)
            else:
                row = lat_ref[sub, r - 2].astype(F32)
            both = jnp.concatenate([row, row], axis=-1)
            shifted[r, 0] = jnp.where(col == 0, 0.0, pltpu.roll(both, 1, 1))
            shifted[r, 1] = both
            shifted[r, 2] = jnp.where(col == 63, 0.0, pltpu.roll(both, 127, 1))
        for pair in range(9):
            parts = []
            for dy in range(3):
                for dx in range(3):
                    parts.append(jnp.where(lane < COLS, shifted[2 * pair + dy, dx], shifted[2 * pair + 1 + dy, dx]))
                    parts.append(zero4)
            parts += [zero4] * 2
            patch[sub, :, pair * LANE:(pair + 1) * LANE] = jnp.concatenate(parts, axis=0).astype(BF16)
        tot = jnp.zeros((8, CH), F32)
        tot_sq = jnp.zeros((8, CH), F32)
        for pair in range(9):
            if pair % 3 == 0:
                total = jnp.dot(wt_ref[...], patch[sub, :, pair * LANE:(pair + 3) * LANE], preferred_element_type=F32)
            lo = (pair % 3) * LANE
            u = (total[:, lo:lo + LANE].T + bias).astype(BF16)
            upper, lower = u[:COLS], u[COLS:]
            if pair == 0:
                halo_a[sub] = upper
            else:
                out_ref[sub, 2 * pair - 1] = upper
            if pair == 8:
                halo_b[sub] = lower
            else:
                out_ref[sub, 2 * pair] = lower
            v = u.astype(F32)
            if pair == 0:
                v = v[COLS:]
            if pair == 8:
                v = v[:COLS]
            tot = tot + fold8(v)
            tot_sq = tot_sq + fold8(v * v)
        sum_ref[pl.ds(sample, 1), :] = tot.sum(axis=0, keepdims=True)
        sq_ref[pl.ds(sample, 1), :] = tot_sq.sum(axis=0, keepdims=True)

    @pl.when(step == samples // 2 - 1)
    def _():
        stats_out[...] = group_sums(sum_ref, sq_ref)


def first_conv(lat, halos, w_in, b_in, time_emb, temb_w, temb_b, peers):
    samples = lat.shape[0]
    return pl.pallas_call(
        functools.partial(first_kernel, peers=peers, samples=samples),
        grid=(samples // 2,),
        in_specs=[pl.BlockSpec((2,) + lat.shape[1:], lambda s: (s, 0, 0, 0))] + [once(a.shape) for a in (halos[0], halos[1], w_in, b_in, time_emb, temb_w, temb_b)],
        out_specs=[
            pl.BlockSpec((2, ROWS, COLS, CH), lambda s: (s, 0, 0, 0)),
            pl.BlockSpec((2, COLS, CH), lambda s: (s, 0, 0)),
            pl.BlockSpec((2, COLS, CH), lambda s: (s, 0, 0)),
            pl.BlockSpec((samples, LANE), lambda s: (0, 0)),
            pl.BlockSpec((2, samples, CH), lambda s: (0, 0, 0)),
        ],
        out_shape=[
            jax.ShapeDtypeStruct((samples, ROWS, COLS, CH), BF16),
            jax.ShapeDtypeStruct((samples, COLS, CH), BF16),
            jax.ShapeDtypeStruct((samples, COLS, CH), BF16),
            jax.ShapeDtypeStruct((samples, LANE), F32),
            jax.ShapeDtypeStruct((2, samples, CH), F32),
        ],
        scratch_shapes=[
            pltpu.VMEM((CH, 80), BF16),
            pltpu.VMEM((2, 80, 18 * COLS), BF16),
            pltpu.VMEM((samples, CH), F32),
            pltpu.VMEM((samples, CH), F32),
        ],
        compiler_params=pltpu.CompilerParams(vmem_limit_bytes=VMEM_LIMIT),
        name="conv_in",
    )(lat, halos[0], halos[1], w_in, b_in, time_emb, temb_w, temb_b)


DOWN_GROUPS = ((0, 2), (2, 2), (4, 4), (8, 8))
DOWN_STEPS = (None, 1, 2, 4)


def down_kernel(x_ref, x_any, bias_ref, w_ref, out_ref, wt_ref, xe, xo, wide, halo, send, recv, *, peers, samples):
    step = pl.program_id(0)
    me = lax.axis_index("sp")

    def group(i):
        first, size = DOWN_GROUPS[i]
        part = pl.ds(first, size)
        return RowSend(x_any.at[part, 15], halo.at[part], send.at[i], recv.at[i], me, peers, 1)

    @pl.when(step == 0)
    def _():
        greet(me, peers)
        for i in range(len(DOWN_GROUPS)):
            group(i).start()
        transpose_weights(w_ref, wt_ref)
        group(0).wait_recv()

    for i in range(1, len(DOWN_GROUPS)):
        @pl.when(step == DOWN_STEPS[i])
        def _():
            group(i).wait_recv()

    bias = bias_ref[...].astype(F32).reshape(1, CH)
    for sub in range(2):
        for r in range(17):
            dst, row0 = (xe, 32 * (r // 2)) if r % 2 == 0 else (xo, 32 * (r // 2))
            for tile, (lo, hi) in enumerate(WIDE):
                v = halo[step * 2 + sub, :, lo:hi] if r == 0 else x_ref[sub, r - 1, :, lo:hi]
                v = v.astype(F32)
                if r == 0:
                    v = jnp.where(me == 0, jnp.zeros_like(v), v)
                slot = (r * 2 + tile) % 8
                parts = []
                for piece in range((hi - lo + 127) // LANE):
                    first, end = piece * LANE, min(hi - lo, piece * LANE + LANE)
                    wide[slot, piece, :, 0:end - first] = v[:, first:end]
                    parts.append([wide[slot, piece, pl.ds(odd, 32, stride=2), 0:end - first] for odd in range(2)])
                even = jnp.concatenate([p[0] for p in parts], axis=-1)
                odd = jnp.concatenate([p[1] for p in parts], axis=-1)
                padded = jnp.concatenate([odd, jnp.zeros((8, hi - lo), F32)], axis=0)
                put_shifted(dst.at[sub], row0, 32, tile, pltpu.roll(padded, 1, 0)[:32], even, odd)
        total = None
        for dy, src in enumerate((xe.at[sub, pl.ds(0, FULL)], xo.at[sub], xe.at[sub, pl.ds(32, FULL)])):
            part = lax.dot_general(wt_ref[dy], src[...], TRANS_B, preferred_element_type=F32)
            total = part if total is None else total + part
        for part in range(2):
            u = (total[:, part * LANE:(part + 1) * LANE].T + bias).astype(BF16)
            out_ref[sub, 4 * part:4 * part + 4] = u.reshape(4, 32, CH)

    @pl.when(step == samples // 2 - 1)
    def _():
        for i in range(len(DOWN_GROUPS)):
            group(i).wait_send()


def down_conv(x, w, bias, peers, collective_id):
    samples = x.shape[0]
    return pl.pallas_call(
        functools.partial(down_kernel, peers=peers, samples=samples),
        grid=(samples // 2,),
        in_specs=[pl.BlockSpec((2, ROWS, COLS, CH), lambda g: (g, 0, 0, 0)), pl.BlockSpec(memory_space=pl.ANY), once(bias.shape), once(w.shape)],
        out_specs=pl.BlockSpec((2, 8, 32, CH), lambda g: (g, 0, 0, 0)),
        out_shape=jax.ShapeDtypeStruct((samples, 8, 32, CH), BF16),
        scratch_shapes=[
            pltpu.VMEM((3, CH, DEEP), BF16),
            pltpu.VMEM((2, 9 * 32, DEEP), BF16),
            pltpu.VMEM((2, 8 * 32, DEEP), BF16),
            pltpu.VMEM((8, 2, COLS, LANE), F32),
            pltpu.VMEM((samples, COLS, CH), BF16),
            pltpu.SemaphoreType.DMA((len(DOWN_GROUPS),)),
            pltpu.SemaphoreType.DMA((len(DOWN_GROUPS),)),
        ],
        compiler_params=pltpu.CompilerParams(vmem_limit_bytes=VMEM_LIMIT, collective_id=collective_id, has_side_effects=True),
        name="down",
    )(x, x, bias, w)


def latent_kernel(lat_ref, halo_a, halo_b, send, recv, *, peers):
    me = lax.axis_index("sp")
    greet(me, peers)
    last = lat_ref.shape[1] - 2
    rows = (
        RowSend(lat_ref.at[:, pl.ds(last, 2)], halo_a, send.at[0], recv.at[0], me, peers, 1),
        RowSend(lat_ref.at[:, pl.ds(0, 2)], halo_b, send.at[1], recv.at[1], me, peers, -1),
    )
    for row in rows:
        row.start()
    for row in rows:
        row.wait_send()
        row.wait_recv()


def latent_halos(lat, peers, collective_id):
    shape = jax.ShapeDtypeStruct((lat.shape[0], 2) + lat.shape[2:], lat.dtype)
    return pl.pallas_call(
        functools.partial(latent_kernel, peers=peers),
        in_specs=[pl.BlockSpec(memory_space=pl.ANY)],
        out_specs=[pl.BlockSpec(memory_space=pl.ANY)] * 2,
        out_shape=[shape, shape],
        scratch_shapes=[pltpu.SemaphoreType.DMA((2,)), pltpu.SemaphoreType.DMA((2,))],
        compiler_params=pltpu.CompilerParams(collective_id=collective_id, has_side_effects=True),
        name="latent_halos",
    )(lat)


def solution(mesh):
    peers = mesh.shape["sp"]

    def band_program(latent, time_emb, w_in, b_in, gn1_scale, gn1_shift, conv1_w, conv1_b, temb_w, temb_b, gn2_scale, gn2_shift, conv2_w, conv2_b, down_w, down_b):
        lat = latent.transpose(0, 1, 3, 2)
        hidden, halo_a, halo_b, stats, embs = first_conv(lat, latent_halos(lat, peers, 0), w_in, b_in, time_emb, temb_w.transpose(0, 2, 1), temb_b, peers)
        outputs = [hidden]
        for i in range(2):
            halos = (halo_a, halo_b) if i == 0 else None
            branch, stats_all, halo_a, halo_b = conv_stage(hidden, halos, stats, gn1_scale, gn1_shift, conv1_b, conv1_w, i, peers, talk=i + 1, emb_out=embs)
            got = conv_stage(branch, (halo_a, halo_b), stats_all, gn2_scale, gn2_shift, conv2_b, conv2_w, i, peers, emb_in=embs, residual=hidden, want_stats=i == 0)
            hidden = got[0]
            stats = got[1] if i == 0 else None
            outputs.append(hidden)
        outputs.append(down_conv(hidden, down_w[None], down_b, peers, 3))
        return tuple(outputs)

    band = P("dp", "sp", None, None)
    return jax.shard_map(band_program, mesh=mesh, in_specs=(band, P("dp", None)) + (P(),) * 14, out_specs=(band,) * 4, check_vma=False)
```

time: 475 us -> 251 us (0.53); the launches traced: 469 us -> 250 us
  matrix products: 260 us -> 0 us
  Pallas kernels: 0 us -> 245 us
  blocking collectives: 71.7 us -> 0 us
  other arithmetic: 47.3 us -> 0 us
  local copies, waits for them, and re-layouts: 44.4 us -> 3.99 us
  starting transfers between devices: 26.5 us -> 0 us
  waiting for transfers between devices: 17.2 us -> 0 us
    conv_general_dilated x6 -> x0, matrix products: 259 us -> none  [conv_valid_rows(): lax.conv_general_dilated(inputs, kernel, (stride, stride), ((0, 0), (1, 1...]
    pallas_call x0 -> x7, Pallas kernels: none -> 245 us  [the longest x4 207 us: conv_stage(): pl.pallas_call(body, grid=(samples // 2,), in_specs=specs, out_specs=out_...]
    psum x4 -> x0, blocking collectives: 71.7 us -> none  [the longest x2 39.2 us: band_program(): sums_all = lax.psum(group_sums(mixed_in), 'sp')]
    convert_element_type x8 -> x0, other arithmetic: 43.4 us -> none  [the longest x4 41.5 us: norm_silu(): jax.nn.silu(values * scale_bc[:, None, None, :] + offset_bc[:, None, None...]
    unnamed x63 -> x1, local copies, waits for them, and re-layouts: 38.1 us -> 3.99 us
    ppermute x11 -> x0, starting transfers between devices: 26.5 us -> none  [the longest x6 20 us: row_from_above(): return lax.ppermute(band_block[:, -1:], 'sp', to_next)]
    ppermute x11 -> x0, waiting for transfers between devices: 17.2 us -> none  [the longest x5 16.5 us: row_from_below(): return lax.ppermute(band_block[:, :1], 'sp', to_prev)]
  transfers between devices with their start and end apart: 11 -> 0, of which waited for: 7 -> 0; matrix products, arithmetic and copies ran while one was open for 7% -> 0% of each run, Pallas kernels for 0% -> 0%
where the time goes in v2:
time: 251 us; the launch traced here: 250 us
  Pallas kernels  245 us (98%)
  local copies, waits for them, and re-layouts  3.99 us (2%)
    pallas_call x4, Pallas kernels, conv_stage(): pl.pallas_call(body, grid=(samples // 2,), in_specs=specs, out_specs=out_...  207 us
    pallas_call x1, Pallas kernels, down_conv(): pl.pallas_call(functools.partial(down_kernel, peers=peers, samples=sample...  18.4 us
    pallas_call x1, Pallas kernels, first_conv(): pl.pallas_call(functools.partial(first_kernel, peers=peers, samples=sampl...  16 us

profile of v2, /device:TPU:0, one launch (start us, length us, event | category | flops | bytes accessed | tf_op | source)
XLA Modules:
  0.0 250.0 jit_solution(17946044848769891355)
XLA Ops:
  0.6 4.3 %latent_halos.1 = (bf16[16,2,4,64]{3,2,1,0:T(4,128)(2,1)}, bf16[16,2,4,64]{3,2,1,0:T(4,128)(2,1)}) custom-call(bf16[16,16,4,64]{3,2,1,0:T(4,128)(2,1)} %bitcast.5), custom_call_target="tpu_custom_call" | custom-call | tf_op jit(solution)/shard_map/latent_halos/pallas_call | solution.py:558
  4.9 16.0 %conv_in.1 = (bf16[16,16,64,320]{3,2,1,0:T(8,128)(2,1)}, bf16[16,64,320]{2,1,0:T(8,128)(2,1)}, bf16[16,64,320]{2,1,0:T(8,128)(2,1)}, f32[16,128]{1,0:T(8,128)}, f32[2,16,320]{2,1,0:T(8,128)}) custom-call(bf16[16,16,4,64]{3,2,1,0:T(4,128)(2,1)} %bitcast.6, bf16[16,2,4,64]{3,2,1,0:T(4,128)(2,1)} %get-tuple-element.21.halo_lat_a, ...), custom_call_target="tpu_custom_call" | custom-call | tf_op jit(solution)/shard_map/conv_in/pallas_call | solution.py:431
  20.9 56.2 %conv_stage_0_1.1 = (bf16[16,16,64,320]{3,2,1,0:T(8,128)(2,1)}, f32[4,16,128]{2,1,0:T(8,128)}, bf16[16,64,320]{2,1,0:T(8,128)(2,1)}, bf16[16,64,320]{2,1,0:T(8,128)(2,1)}) custom-call(bf16[16,16,64,320]{3,2,1,0:T(8,128)(2,1)} %get-tuple-element.42.refs_0_.refs_1_.refs_2_.refs_11_, ...), custom_call_target="tpu_custom_call" | custom-call | tf_op jit(solution)/shard_map/conv_stage_0_1/pallas_call | solution.py:340
  77.2 49.6 %conv_stage_0_2.1 = (bf16[16,16,64,320]{3,2,1,0:T(8,128)(2,1)}, f32[16,128]{1,0:T(8,128)}) custom-call(bf16[16,16,64,320]{3,2,1,0:T(8,128)(2,1)} %get-tuple-element.28.refs_0_.refs_1_.refs_2_, bf16[16,16,64,320]{3,2,1,0:T(8,128)(2,1)} %get-tuple-element.28.refs_0_.refs_1_.refs_2_, bf16[16,16,64,320]{3,2,1,0:T(8,128)(2,1)} %get-tuple-element.28.refs_0_.refs_1_.refs_2_, ...), custom_call_target="tpu_custom_call" | custom-call | tf_op jit(solution)/shard_map/conv_stage_0_2/pallas_call | solution.py:340
  126.7 54.3 %conv_stage_1_1.1 = (bf16[16,16,64,320]{3,2,1,0:T(8,128)(2,1)}, f32[4,16,128]{2,1,0:T(8,128)}, bf16[16,64,320]{2,1,0:T(8,128)(2,1)}, bf16[16,64,320]{2,1,0:T(8,128)(2,1)}) custom-call(bf16[16,16,64,320]{3,2,1,0:T(8,128)(2,1)} %get-tuple-element.43.refs_0_.refs_1_.refs_2_.refs_3_.refs_11_, ...), custom_call_target="tpu_custom_call" | custom-call | tf_op jit(solution)/shard_map/conv_stage_1_1/pallas_call | solution.py:340
  181.0 46.6 %conv_stage_1_2.1.x_ref.x_any = bf16[16,16,64,320]{3,2,1,0:T(8,128)(2,1)} custom-call(bf16[16,16,64,320]{3,2,1,0:T(8,128)(2,1)} %get-tuple-element.34.refs_0_.refs_1_.refs_2_, bf16[16,16,64,320]{3,2,1,0:T(8,128)(2,1)} %get-tuple-element.34.refs_0_.refs_1_.refs_2_, bf16[16,16,64,320]{3,2,1,0:T(8,128)(2,1)} %get-tuple-element.34.refs_0_.refs_1_.refs_2_, ...), custom_call_target="tpu_custom_call" | custom-call | tf_op jit(solution)/shard_map/conv_stage_1_2/pallas_call | solution.py:340
  227.6 18.4 %down.1 = bf16[16,8,32,320]{3,2,1,0:T(8,128)(2,1)} custom-call(bf16[16,16,64,320]{3,2,1,0:T(8,128)(2,1)} %conv_stage_1_2.1.x_ref.x_any, bf16[16,16,64,320]{3,2,1,0:T(8,128)(2,1)} %conv_stage_1_2.1.x_ref.x_any, bf16[320]{0:T(512)(128)(2,1)} %bias_ref.1, bf16[1,3,3,320,320]{4,3,2,1,0:T(8,128)(2,1)} %bitcast.3), custom_call_target="tpu_custom_call" | custom-call | tf_op jit(solution)/shard_map/down/pallas_call | solution.py:521
  246.0 4.0 %copy.21 = bf16[16,8,32,320]{3,2,1,0:T(8,128)(2,1)} copy(bf16[16,8,32,320]{3,2,1,0:T(8,128)(2,1)} %down.1) | data formatting | bytes 5242880
